TPU v7x, 128 devices: a whole 4x4x4 slice. The times are simulated.
128 devices in a mesh: row: 16 (over y, z), col: 8 (over x, core).
Axes of the slice: x: 4, y: 4, z: 4, core: 2. Of those that a mesh axis runs over, the one named last changes fastest.
Arguments:
- conductance: float32 [512, 4096], P('row', 'col'), may hold values from 0.1 to 10
- nodata_mask: int32 [512, 4096], P('row', 'col'), may hold values 0 or 1
- source_index: int32 [16, 16], replicated, may hold values from 0 to 2097151
- source_current: float32 [16, 16], replicated, may hold values from 1 to 10
- ground_index: int32 [16, 16], replicated, may hold values from 0 to 2097151
Outputs:
- voltage: float32 [16, 512, 4096], P(None, 'row', 'col')
Inputs may be any that keep to these rules, and one draw needn't show every extreme that they name: `source_index`: each source's row is its index // 4096 and its column its index % 4096; indices may repeat and may name nodata cells. `ground_index`: read as source_index; a ground on a nodata cell still counts.
All inputs are finite; a program needn't handle non-finite values. No bound on the sum of `nodata_mask` on one device may be relied on, other than what follows from the above.
Results may differ from a plain program's by a relative error of at most 0.0003.
Values sent between devices are 32-bit elements; how exact they have to be, the bound alone decides.
A program may use at most 64 MiB of HBM per device.

v0:
```python
import jax
import jax.numpy as jnp
from jax import lax
from jax.sharding import Mesh
from jax.sharding import PartitionSpec as P

SWEEPS = 5
ITERS = 3
ROW_COL = ("row_0", "row_1", "col_0", "col_1")
ROW = ("row_0", "row_1")
COL = ("col_0", "col_1")


LEAKAGE = 0.0001
GROUND_CONDUCTANCE = 1.0
RELAXATION = 2.0 / 3.0


def padded_2(block, sides, width):
    for axis, dim in sides:
        count = lax.axis_size(axis)
        forward = [(i, i + 1) for i in range(count - 1)]
        backward = [(target, source) for source, target in forward]
        low = lax.ppermute(
            lax.slice_in_dim(block, block.shape[dim] - width, None, axis=dim), axis, forward
        )
        high = lax.ppermute(lax.slice_in_dim(block, 0, width, axis=dim), axis, backward)
        block = jnp.concatenate([low, block, high], axis=dim)
    return block


def from_everyone(x, axis):
    copies = jnp.broadcast_to(x, (lax.axis_size(axis), *x.shape))
    return lax.all_to_all(copies, axis, split_axis=0, concat_axis=0, tiled=True)


def laid_out(pieces, dim):
    pieces = jnp.moveaxis(pieces, 0, dim)
    shape = pieces.shape
    return pieces.reshape(*shape[:dim], shape[dim] * shape[dim + 1], *shape[dim + 2 :])


def whole_of(x, axes, dim):
    far, near = axes
    pieces = from_everyone(from_everyone(x, far), near)
    return laid_out(pieces.swapaxes(0, 1).reshape(-1, *x.shape), dim)


def over_copies(x, axis):
    everything = from_everyone(x, axis)
    return jnp.sum(everything, axis=0)


def one_axis_at_a_time(x, axes):
    far, near = axes
    return over_copies(over_copies(x, near), far)


def rows_first(arrays, axis, dims):
    turned = [jnp.moveaxis(a, dim, 0) for a, dim in zip(arrays, dims)]
    widths = [t[0].size for t in turned]
    both = jnp.concatenate([t.reshape(-1, w) for t, w in zip(turned, widths)], axis=1)
    out = lax.all_gather(both, axis, axis=0, tiled=True)
    pieces = jnp.split(out, [sum(widths[:k]) for k in range(1, len(widths))], axis=1)
    return tuple(
        (
            jnp.moveaxis(b.reshape(-1, *t.shape[1:]), 0, dim)
            for b, t, dim in zip(pieces, turned, dims)
        )
    )


def extended(x, sides, width):
    edges = {}
    for axis, dim in sides:
        size, length = (lax.axis_size(axis), x.shape[dim])
        up = [(i, (i + 1) % size) for i in range(size - 1)]
        last = lax.slice_in_dim(x, length - width, length, axis=dim)
        leading = lax.slice_in_dim(x, 0, width, axis=dim)
        edges[dim] = (
            lax.ppermute(last, axis, up),
            lax.ppermute(leading, axis, [(b, a) for a, b in up]),
        )
    done = []
    for _, dim in sides:
        low, high = edges[dim]
        around = [(width, width) if d in done else (0, 0) for d in range(x.ndim)]
        x = jnp.concatenate([jnp.pad(low, around), x, jnp.pad(high, around)], axis=dim)
        done.append(dim)
    return x


def window(array, margin, height, breadth):
    return array[..., margin : margin + height, margin : margin + breadth]


def apply_operator(field, width, coeffs):
    diagonal, inverse, east_edge, south_edge, tile_rows, tile_cols = coeffs
    narrow = width - 1
    height = tile_rows + 2 * narrow
    breadth = tile_cols + 2 * narrow
    diag_margin = (diagonal.shape[-2] - tile_rows) // 2
    start = (east_edge.shape[-2] - tile_rows) // 2 - narrow
    diag_now = window(diagonal, diag_margin - narrow, height, breadth)
    east_here = east_edge[start : start + height, start : start + breadth]
    east_west = east_edge[start : start + height, start - 1 : start - 1 + breadth]
    south_here = south_edge[start : start + height, start : start + breadth]
    south_north = south_edge[start - 1 : start - 1 + height, start : start + breadth]
    return (
        diag_now * field[:, 1:-1, 1:-1]
        - east_here * field[:, 1:-1, 2:]
        - east_west * field[:, 1:-1, :-2]
        - south_here * field[:, 2:, 1:-1]
        - south_north * field[:, :-2, 1:-1]
    )


def smooth(residual, coeffs):
    diagonal, inverse, east_edge, south_edge, tile_rows, tile_cols = coeffs
    margin = (inverse.shape[-2] - tile_rows) // 2
    reach = SWEEPS - 1
    wide = padded_2(residual, ((ROW, 1), (COL, 2)), reach)
    iterate = (
        RELAXATION
        * window(inverse, margin - reach, tile_rows + 2 * reach, tile_cols + 2 * reach)
        * wide
    )
    for sweep_step in range(SWEEPS - 1):
        width = reach - sweep_step
        narrow = width - 1
        height = tile_rows + 2 * narrow
        breadth = tile_cols + 2 * narrow
        target = window(wide, sweep_step + 1, height, breadth)
        iterate = window(iterate, 1, height, breadth) + RELAXATION * window(
            inverse, margin - narrow, height, breadth
        ) * (target - apply_operator(iterate, width, coeffs))
    return iterate


def coarse_solve(factor, rhs):
    forward = lax.linalg.triangular_solve(factor, rhs, left_side=True, lower=True)
    return lax.linalg.triangular_solve(
        factor, forward, left_side=True, lower=True, transpose_a=True
    )


def block_sums(field):
    return jnp.sum(field, axis=(1, 2))


def gather_sums(field):
    return whole_of(block_sums(field)[None], (("row_0", "row_1", "col_0"), "col_1"), 0)


def inner_energy(residual, precond):
    return one_axis_at_a_time(
        jnp.sum(residual * precond, axis=(1, 2)), (("row_0", "row_1", "col_0"), "col_1")
    )


def shards(conductance, nodata_mask, source_index, source_current, ground_index):
    tile_rows, tile_cols = conductance.shape
    row_devices = lax.axis_size(ROW)
    col_devices = lax.axis_size(COL)
    total_cols = tile_cols * col_devices
    margin = SWEEPS + 2
    reach = SWEEPS
    present_tile = nodata_mask.astype(jnp.float32)
    fields = jnp.stack([conductance * present_tile, present_tile])
    padded = padded_2(fields, ((ROW, 1), (COL, 2)), margin)
    masked = padded[0]
    present = padded[1]
    east_edge = (
        0.5 * present[1:-1, 1:-1] * present[1:-1, 2:] * (masked[1:-1, 1:-1] + masked[1:-1, 2:])
    )
    south_edge = (
        0.5 * present[1:-1, 1:-1] * present[2:, 1:-1] * (masked[1:-1, 1:-1] + masked[2:, 1:-1])
    )
    base = (
        east_edge[1:-1, 1:-1]
        + east_edge[1:-1, :-2]
        + south_edge[1:-1, 1:-1]
        + south_edge[:-2, 1:-1]
        + LEAKAGE
    )
    row_coords = (
        lax.axis_index(ROW) * tile_rows - reach + jnp.arange(tile_rows + 2 * reach, dtype=jnp.int32)
    )
    col_coords = (
        lax.axis_index(COL) * tile_cols - reach + jnp.arange(tile_cols + 2 * reach, dtype=jnp.int32)
    )
    ground_rows = ground_index // total_cols
    ground_cols = ground_index % total_cols
    ground_row_hits = (row_coords[None, None, :] == ground_rows[:, :, None]).astype(jnp.float32)
    ground_col_hits = (col_coords[None, None, :] == ground_cols[:, :, None]).astype(jnp.float32)
    shunt = GROUND_CONDUCTANCE * jnp.einsum(
        "bki,bkj->bij", ground_row_hits, ground_col_hits, precision=lax.Precision.HIGHEST
    )
    diagonal = base[None] + shunt
    inverse = 1.0 / diagonal
    inner_rows = row_coords[reach : reach + tile_rows]
    inner_cols = col_coords[reach : reach + tile_cols]
    source_rows = source_index // total_cols
    source_cols = source_index % total_cols
    source_row_hits = (inner_rows[None, None, :] == source_rows[:, :, None]).astype(
        jnp.float32
    ) * source_current[:, :, None]
    source_col_hits = (inner_cols[None, None, :] == source_cols[:, :, None]).astype(jnp.float32)
    inflow = (
        jnp.einsum(
            "bki,bkj->bij", source_row_hits, source_col_hits, precision=lax.Precision.HIGHEST
        )
        * present_tile[None]
    )
    edge_margin = reach + 1
    east_cross = jnp.sum(
        east_edge[edge_margin : edge_margin + tile_rows, edge_margin + tile_cols - 1]
    )
    south_cross = jnp.sum(
        south_edge[edge_margin + tile_rows - 1, edge_margin : edge_margin + tile_cols]
    )
    shunt_total = LEAKAGE * tile_rows * tile_cols + jnp.sum(
        window(shunt, reach, tile_rows, tile_cols), axis=(1, 2)
    )
    east_all, south_all, shunt_all = rows_first(
        (east_cross[None], south_cross[None], shunt_total[None]), ROW_COL, (0, 0, 0)
    )
    east_grid = east_all.reshape(row_devices, col_devices)
    south_grid = south_all.reshape(row_devices, col_devices)
    east_west = jnp.pad(east_grid[:, :-1], ((0, 0), (1, 0))).reshape(-1)
    south_north = jnp.pad(south_grid[:-1], ((1, 0), (0, 0))).reshape(-1)
    degree = (
        shunt_all
        + east_all[:, None]
        + east_west[:, None]
        + south_all[:, None]
        + south_north[:, None]
    )
    coupling = (
        jnp.diag(east_all[:-1], 1)
        + jnp.diag(east_all[:-1], -1)
        + jnp.diag(south_all[:-col_devices], col_devices)
        + jnp.diag(south_all[:-col_devices], -col_devices)
    )
    block_count = east_all.shape[0]
    coarse_matrix = (
        degree.T[:, :, None] * jnp.eye(block_count, dtype=jnp.float32)[None] - coupling[None]
    )
    factor = jnp.linalg.cholesky(coarse_matrix)
    coarse_index = lax.axis_index(ROW) * col_devices + lax.axis_index(COL)
    coeffs = (diagonal, inverse, east_edge, south_edge, tile_rows, tile_cols)

    def precondition(residual, coarse_rhs):
        solved = coarse_solve(factor, coarse_rhs.T[:, :, None])[:, :, 0]
        own_value = lax.dynamic_index_in_dim(solved, coarse_index, 1, keepdims=False)
        return smooth(residual, coeffs) + own_value[:, None, None]

    voltage = jnp.zeros_like(inflow)
    residual = inflow
    precond = precondition(residual, gather_sums(residual))
    direction = precond
    energy = inner_energy(residual, precond)
    for iteration_step in range(ITERS):
        wide = extended(direction, ((ROW, 1), (COL, 2)), 1)
        image = apply_operator(wide, 1, coeffs)
        alpha = energy / one_axis_at_a_time(
            jnp.sum(direction * image, axis=(1, 2)), (("row_0", "row_1", "col_0"), "col_1")
        )
        coarse_rhs = None
        voltage = voltage + alpha[:, None, None] * direction
        if iteration_step + 1 < ITERS:
            residual = residual - alpha[:, None, None] * image
            coarse_rhs = gather_sums(residual)
            precond = precondition(residual, coarse_rhs)
            energy_next = inner_energy(residual, precond)
            direction = precond + (energy_next / energy)[:, None, None] * direction
            energy = energy_next
    return voltage


def solution(mesh):
    split = Mesh(mesh.devices.reshape(4, 4, 4, 2), ("row_0", "row_1", "col_0", "col_1"))
    return jax.shard_map(
        shards,
        mesh=split,
        in_specs=(P(ROW, COL), P(ROW, COL), P(), P(), P()),
        out_specs=P(None, ROW, COL),
        check_vma=False,
    )
```

profile of v0, /device:TPU:1, one launch (start us, length us, event | category | flops | bytes accessed | tf_op | source)
XLA Modules:
  0.0 772.0 jit_solution(8758683497485463415)
XLA Ops:
  1.8 4.4 collective-permute-start
  10.7 11.6 %all-to-all-start = ((f32[64,1,16]{2,1,0:T(1,128)}), f32[64,1,16]{2,1,0:T(1,128)S(1)}, u32[]{:S(2)}, u32[]{:S(2)}) async-start(f32[64,1,16]{2,1,0:T(1,128)} %broadcast_in_dim.123), calls=%async_computation | async-start | bytes 65536 | tf_op jit(solution)/shard_map/all_to_all | solution.py:34
  30.8 6.0 all_to_all.111
  54.9 30.3 %all-gather = f32[128,1,18]{2,1,0:T(1,128)S(1)} all-gather(f32[1,1,18]{2,1,0:T(1,128)S(1)} %maximum_bitcast_fusion), channel_id=1, replica_groups=mesh['row_0'=4,'row_1'=4,'col_0'=4,'col_1'=2] {'row_0','row_1','col_0','..., dimensions={0}, use_global_device_ids=true | all-gather | bytes 9288 | tf_op jit(solution)/shard_map/all_gather | solution.py:63
  87.4 189.0 %custom-call.10 = f32[16,128,128]{2,1,0:T(8,128)} custom-call(f32[16,128,128]{2,1,0:T(8,128)} %add_multiply_fusion), custom_call_target="Cholesky" | custom-call | tf_op jit(solution)/shard_map/jit(cholesky)/cholesky | solution.py:249
  279.1 158.6 %custom-call.16 = f32[16,1,128,128]{2,3,1,0:T(8,128)} custom-call(f32[16,1,128,128]{3,2,1,0:T(8,128)} %select_bitcast_fusion), custom_call_target="InvertDiagBlocksLowerTriangular" | custom-call | tf_op jit(solution)/shard_map/triangular_solve/custom-call.2 | solution.py:142
  451.6 4.4 collective-permute-done.7
  473.1 4.0 collective-permute-start.8
  497.6 10.5 %all-to-all-start.5 = ((f32[64,1,16]{2,1,0:T(1,128)}), f32[64,1,16]{2,1,0:T(1,128)S(1)}, u32[]{:S(2)}, u32[]{:S(2)}) async-start(f32[64,1,16]{2,1,0:T(1,128)} %broadcast_in_dim.238), calls=%async_computation.5 | async-start | bytes 65536 | tf_op jit(solution)/shard_map/all_to_all | solution.py:34
  508.1 8.4 %all-to-all-done.5 = f32[64,1,16]{2,1,0:T(1,128)S(1)} async-done(((f32[64,1,16]{2,1,0:T(1,128)}), f32[64,1,16]{2,1,0:T(1,128)S(1)}, u32[]{:S(2)}, u32[]{:S(2)}) %all-to-all-start.5) | async-done | bytes 4128 | tf_op jit(solution)/shard_map/all_to_all | solution.py:34
  517.2 4.7 all-to-all-start.3
  521.9 8.3 %all-to-all-done.3 = f32[64,1,16]{2,1,0:T(1,128)S(1)} async-done(((f32[64,1,16]{2,1,0:T(1,128)}), f32[64,1,16]{2,1,0:T(1,128)S(1)}, u32[]{:S(2)}, u32[]{:S(2)}) %all-to-all-start.3) | async-done | bytes 4128 | tf_op jit(solution)/shard_map/all_to_all | solution.py:34
  533.9 4.7 all-to-all-start.6
  547.2 7.9 %all_to_all.113 = f32[2,1,1024]{2,1,0:T(1,128)S(1)} all-to-all(f32[2,1,1024]{2,1,0:T(1,128)S(1)} %reshape.343), channel_id=1, replica_groups=mesh['row_0'=4,'row_1'=4,'col_0'=4,'col_1'=2] {'col_1'}, dimensions={0} | all-to-all | bytes 16384 | tf_op jit(solution)/shard_map/all_to_all | solution.py:34
  570.1 4.4 collective-permute-done.15
  594.1 17.2 %all_to_all.115 = f32[64,1,16]{2,1,0:T(1,128)S(1)} all-to-all(f32[64,1,16]{2,1,0:T(1,128)S(1)} %broadcast_in_dim.243), channel_id=1, replica_groups=mesh['row_0'=4,'row_1'=4,'col_0'=4,'col_1'=2] {'row_0','row_1','col_0'}, dimensions={0} | all-to-all | bytes 8192 | tf_op jit(solution)/shard_map/all_to_all | solution.py:34
  619.4 4.2 collective-permute-start.18
  634.8 17.2 %all_to_all.117 = f32[64,1,16]{2,1,0:T(1,128)S(1)} all-to-all(f32[64,1,16]{2,1,0:T(1,128)S(1)} %broadcast_in_dim.245), channel_id=1, replica_groups=mesh['row_0'=4,'row_1'=4,'col_0'=4,'col_1'=2] {'row_0','row_1','col_0'}, dimensions={0} | all-to-all | bytes 8192 | tf_op jit(solution)/shard_map/all_to_all | solution.py:34
  655.5 4.7 all-to-all-start.12
  668.8 6.5 all_to_all.118
  688.9 4.4 collective-permute-done.23
  713.0 17.2 %all_to_all.120 = f32[64,1,16]{2,1,0:T(1,128)S(1)} all-to-all(f32[64,1,16]{2,1,0:T(1,128)S(1)} %broadcast_in_dim.250), channel_id=1, replica_groups=mesh['row_0'=4,'row_1'=4,'col_0'=4,'col_1'=2] {'row_0','row_1','col_0'}, dimensions={0} | all-to-all | bytes 8192 | tf_op jit(solution)/shard_map/all_to_all | solution.py:34
  737.3 4.4 collective-permute-start.26
  751.9 17.2 %all_to_all.122 = f32[64,1,16]{2,1,0:T(1,128)S(1)} all-to-all(f32[64,1,16]{2,1,0:T(1,128)S(1)} %broadcast_in_dim.252), channel_id=1, replica_groups=mesh['row_0'=4,'row_1'=4,'col_0'=4,'col_1'=2] {'row_0','row_1','col_0'}, dimensions={0} | all-to-all | bytes 8192 | tf_op jit(solution)/shard_map/all_to_all | solution.py:34
  (314 shorter events, 220.3 us)
Async XLA Ops:
  1.8 36.4 %collective-permute-start = (f32[2,7,512]{2,1,0:T(8,128)S(1)}, f32[2,7,512]{2,1,0:T(8,128)S(1)}, u32[]{:S(2)}, u32[]{:S(2)}) collective-permute-start(f32[2,7,512]{2,1,0:T(8,128)S(1)} %get-tuple-element.58), channel_id=1, source_target_pairs={{0,8},{8,16},{16,24},{24,32},{32,40},{40,48},{48,56},{56,64},{64,7... | collective-permute-start | bytes 86024 | tf_op jit(solution)/shard_map/ppermute | solution.py:24
  6.1 32.0 %collective-permute-start.1 = (f32[2,7,512]{2,1,0:T(8,128)S(1)}, f32[2,7,512]{2,1,0:T(8,128)S(1)}, u32[]{:S(2)}, u32[]{:S(2)}) collective-permute-start(f32[2,7,512]{2,1,0:T(8,128)S(1)} %get-tuple-element.59), channel_id=1, source_target_pairs={{8,0},{16,8},{24,16},{32,24},{40,32},{48,40},{56,48},{64,56},{72,6... | collective-permute-start | bytes 86024 | tf_op jit(solution)/shard_map/ppermute | solution.py:27
  10.7 20.0 %all-to-all-start = ((f32[64,1,16]{2,1,0:T(1,128)}), f32[64,1,16]{2,1,0:T(1,128)S(1)}, u32[]{:S(2)}, u32[]{:S(2)}) async-start(f32[64,1,16]{2,1,0:T(1,128)} %broadcast_in_dim.123), calls=%async_computation | async-start | bytes 65536 | tf_op jit(solution)/shard_map/all_to_all | solution.py:34
  23.1 420.7 %collective-permute-start.4 = (f32[16,4,512]{2,1,0:T(4,128)}, f32[16,4,512]{2,1,0:T(4,128)}, u32[]{:S(2)}, u32[]{:S(2)}) collective-permute-start(f32[16,4,512]{2,1,0:T(4,128)} %get-tuple-element.50), channel_id=1, source_target_pairs={{0,8},{8,16},{16,24},{24,32},{32,40},{40,48},{48,56},{56,64},{64,7... | collective-permute-start | bytes 393224 | tf_op jit(solution)/shard_map/ppermute | solution.py:24
  26.6 417.1 %collective-permute-start.5 = (f32[16,4,512]{2,1,0:T(4,128)}, f32[16,4,512]{2,1,0:T(4,128)}, u32[]{:S(2)}, u32[]{:S(2)}) collective-permute-start(f32[16,4,512]{2,1,0:T(4,128)} %get-tuple-element.51), channel_id=1, source_target_pairs={{8,0},{16,8},{24,16},{32,24},{40,32},{48,40},{56,48},{64,56},{72,6... | collective-permute-start | bytes 393224 | tf_op jit(solution)/shard_map/ppermute | solution.py:27
  447.6 8.4 %collective-permute-start.7 = (f32[16,40,4]{2,1,0:T(8,128)S(1)}, f32[16,40,4]{2,1,0:T(8,128)S(1)}, u32[]{:S(2)}, u32[]{:S(2)}) collective-permute-start(f32[16,40,4]{2,1,0:T(8,128)S(1)} %get-tuple-element.33), channel_id=1, source_target_pairs={{1,0},{2,1},{3,2},{4,3},{5,4},{6,5},{7,6},{9,8},{10,9},{11,10},{12... | collective-permute-start | bytes 30728 | tf_op jit(solution)/shard_map/ppermute | solution.py:27
  471.8 14.3 %collective-permute-start.9 = (f32[16,1,512]{2,1,0:T(1,128)S(1)}, f32[16,1,512]{2,1,0:T(1,128)S(1)}, u32[]{:S(2)}, u32[]{:S(2)}) collective-permute-start(f32[16,1,512]{2,1,0:T(1,128)S(1)} %get-tuple-element.48), channel_id=1, source_target_pairs={{8,0},{16,8},{24,16},{32,24},{40,32},{48,40},{56,48},{64,56},{72,6... | collective-permute-start | bytes 98312 | tf_op jit(solution)/shard_map/ppermute | solution.py:82
  473.1 13.0 %collective-permute-start.8 = (f32[16,1,512]{2,1,0:T(1,128)S(1)}, f32[16,1,512]{2,1,0:T(1,128)S(1)}, u32[]{:S(2)}, u32[]{:S(2)}) collective-permute-start(f32[16,1,512]{2,1,0:T(1,128)S(1)} %get-tuple-element.49), channel_id=1, source_target_pairs={{0,8},{8,16},{16,24},{24,32},{32,40},{40,48},{48,56},{56,64},{64,7... | collective-permute-start | bytes 98312 | tf_op jit(solution)/shard_map/ppermute | solution.py:81
  497.6 18.9 %all-to-all-start.5 = ((f32[64,1,16]{2,1,0:T(1,128)}), f32[64,1,16]{2,1,0:T(1,128)S(1)}, u32[]{:S(2)}, u32[]{:S(2)}) async-start(f32[64,1,16]{2,1,0:T(1,128)} %broadcast_in_dim.238), calls=%async_computation.5 | async-start | bytes 65536 | tf_op jit(solution)/shard_map/all_to_all | solution.py:34
  517.2 13.1 %all-to-all-start.3 = ((f32[64,1,16]{2,1,0:T(1,128)}), f32[64,1,16]{2,1,0:T(1,128)S(1)}, u32[]{:S(2)}, u32[]{:S(2)}) async-start(f32[64,1,16]{2,1,0:T(1,128)} %broadcast_in_dim.127), calls=%async_computation.3 | async-start | bytes 65536 | tf_op jit(solution)/shard_map/all_to_all | solution.py:34
  533.9 13.1 %all-to-all-start.6 = ((f32[64,1,16]{2,1,0:T(1,128)}), f32[64,1,16]{2,1,0:T(1,128)S(1)}, u32[]{:S(2)}, u32[]{:S(2)}) async-start(f32[64,1,16]{2,1,0:T(1,128)} %broadcast_in_dim.239), calls=%async_computation.6 | async-start | bytes 65536 | tf_op jit(solution)/shard_map/all_to_all | solution.py:34
  540.4 21.8 %collective-permute-start.12 = (f32[16,4,512]{2,1,0:T(4,128)}, f32[16,4,512]{2,1,0:T(4,128)}, u32[]{:S(2)}, u32[]{:S(2)}) collective-permute-start(f32[16,4,512]{2,1,0:T(4,128)} %get-tuple-element.44), channel_id=1, source_target_pairs={{0,8},{8,16},{16,24},{24,32},{32,40},{40,48},{48,56},{56,64},{64,7... | collective-permute-start | bytes 393224 | tf_op jit(solution)/shard_map/ppermute | solution.py:24
  544.0 18.2 %collective-permute-start.13 = (f32[16,4,512]{2,1,0:T(4,128)}, f32[16,4,512]{2,1,0:T(4,128)}, u32[]{:S(2)}, u32[]{:S(2)}) collective-permute-start(f32[16,4,512]{2,1,0:T(4,128)} %get-tuple-element.45), channel_id=1, source_target_pairs={{8,0},{16,8},{24,16},{32,24},{40,32},{48,40},{56,48},{64,56},{72,6... | collective-permute-start | bytes 393224 | tf_op jit(solution)/shard_map/ppermute | solution.py:27
  566.1 8.4 %collective-permute-start.15 = (f32[16,40,4]{2,1,0:T(8,128)S(1)}, f32[16,40,4]{2,1,0:T(8,128)S(1)}, u32[]{:S(2)}, u32[]{:S(2)}) collective-permute-start(f32[16,40,4]{2,1,0:T(8,128)S(1)} %get-tuple-element.31), channel_id=1, source_target_pairs={{1,0},{2,1},{3,2},{4,3},{5,4},{6,5},{7,6},{9,8},{10,9},{11,10},{12... | collective-permute-start | bytes 30728 | tf_op jit(solution)/shard_map/ppermute | solution.py:27
  613.9 15.1 %collective-permute-start.17 = (f32[16,1,512]{2,1,0:T(1,128)S(1)}, f32[16,1,512]{2,1,0:T(1,128)S(1)}, u32[]{:S(2)}, u32[]{:S(2)}) collective-permute-start(f32[16,1,512]{2,1,0:T(1,128)S(1)} %get-tuple-element.42), channel_id=1, source_target_pairs={{8,0},{16,8},{24,16},{32,24},{40,32},{48,40},{56,48},{64,56},{72,6... | collective-permute-start | bytes 98312 | tf_op jit(solution)/shard_map/ppermute | solution.py:82
  615.2 13.8 %collective-permute-start.16 = (f32[16,1,512]{2,1,0:T(1,128)S(1)}, f32[16,1,512]{2,1,0:T(1,128)S(1)}, u32[]{:S(2)}, u32[]{:S(2)}) collective-permute-start(f32[16,1,512]{2,1,0:T(1,128)S(1)} %get-tuple-element.43), channel_id=1, source_target_pairs={{0,8},{8,16},{16,24},{24,32},{32,40},{40,48},{48,56},{56,64},{64,7... | collective-permute-start | bytes 98312 | tf_op jit(solution)/shard_map/ppermute | solution.py:81
  619.4 8.5 %collective-permute-start.18 = (f32[16,32,1]{2,1,0:T(8,128)S(1)}, f32[16,32,1]{2,1,0:T(8,128)S(1)}, u32[]{:S(2)}, u32[]{:S(2)}) collective-permute-start(f32[16,32,1]{2,1,0:T(8,128)S(1)} %get-tuple-element.40), channel_id=1, source_target_pairs={{1,0},{2,1},{3,2},{4,3},{5,4},{6,5},{7,6},{9,8},{10,9},{11,10},{12... | collective-permute-start | bytes 6152 | tf_op jit(solution)/shard_map/ppermute | solution.py:82
  655.5 13.2 %all-to-all-start.12 = ((f32[64,1,16]{2,1,0:T(1,128)}), f32[64,1,16]{2,1,0:T(1,128)S(1)}, u32[]{:S(2)}, u32[]{:S(2)}) async-start(f32[64,1,16]{2,1,0:T(1,128)} %broadcast_in_dim.246), calls=%async_computation.12 | async-start | bytes 65536 | tf_op jit(solution)/shard_map/all_to_all | solution.py:34
  662.0 19.2 %collective-permute-start.20 = (f32[16,4,512]{2,1,0:T(4,128)}, f32[16,4,512]{2,1,0:T(4,128)}, u32[]{:S(2)}, u32[]{:S(2)}) collective-permute-start(f32[16,4,512]{2,1,0:T(4,128)} %get-tuple-element.38), channel_id=1, source_target_pairs={{0,8},{8,16},{16,24},{24,32},{32,40},{40,48},{48,56},{56,64},{64,7... | collective-permute-start | bytes 393224 | tf_op jit(solution)/shard_map/ppermute | solution.py:24
  665.5 15.6 %collective-permute-start.21 = (f32[16,4,512]{2,1,0:T(4,128)}, f32[16,4,512]{2,1,0:T(4,128)}, u32[]{:S(2)}, u32[]{:S(2)}) collective-permute-start(f32[16,4,512]{2,1,0:T(4,128)} %get-tuple-element.39), channel_id=1, source_target_pairs={{8,0},{16,8},{24,16},{32,24},{40,32},{48,40},{56,48},{64,56},{72,6... | collective-permute-start | bytes 393224 | tf_op jit(solution)/shard_map/ppermute | solution.py:27
  684.9 8.4 %collective-permute-start.23 = (f32[16,40,4]{2,1,0:T(8,128)S(1)}, f32[16,40,4]{2,1,0:T(8,128)S(1)}, u32[]{:S(2)}, u32[]{:S(2)}) collective-permute-start(f32[16,40,4]{2,1,0:T(8,128)S(1)} %get-tuple-element.29), channel_id=1, source_target_pairs={{1,0},{2,1},{3,2},{4,3},{5,4},{6,5},{7,6},{9,8},{10,9},{11,10},{12... | collective-permute-start | bytes 30728 | tf_op jit(solution)/shard_map/ppermute | solution.py:27
  731.8 15.2 %collective-permute-start.25 = (f32[16,1,512]{2,1,0:T(1,128)S(1)}, f32[16,1,512]{2,1,0:T(1,128)S(1)}, u32[]{:S(2)}, u32[]{:S(2)}) collective-permute-start(f32[16,1,512]{2,1,0:T(1,128)S(1)} %get-tuple-element.36), channel_id=1, source_target_pairs={{8,0},{16,8},{24,16},{32,24},{40,32},{48,40},{56,48},{64,56},{72,6... | collective-permute-start | bytes 98312 | tf_op jit(solution)/shard_map/ppermute | solution.py:82
  733.1 13.9 %collective-permute-start.24 = (f32[16,1,512]{2,1,0:T(1,128)S(1)}, f32[16,1,512]{2,1,0:T(1,128)S(1)}, u32[]{:S(2)}, u32[]{:S(2)}) collective-permute-start(f32[16,1,512]{2,1,0:T(1,128)S(1)} %get-tuple-element.37), channel_id=1, source_target_pairs={{0,8},{8,16},{16,24},{24,32},{32,40},{40,48},{48,56},{56,64},{64,7... | collective-permute-start | bytes 98312 | tf_op jit(solution)/shard_map/ppermute | solution.py:81
  737.3 8.6 %collective-permute-start.26 = (f32[16,32,1]{2,1,0:T(8,128)S(1)}, f32[16,32,1]{2,1,0:T(8,128)S(1)}, u32[]{:S(2)}, u32[]{:S(2)}) collective-permute-start(f32[16,32,1]{2,1,0:T(8,128)S(1)} %get-tuple-element.34), channel_id=1, source_target_pairs={{1,0},{2,1},{3,2},{4,3},{5,4},{6,5},{7,6},{9,8},{10,9},{11,10},{12... | collective-permute-start | bytes 6152 | tf_op jit(solution)/shard_map/ppermute | solution.py:82
  (62 other events, 531.6 us)
where the time goes:
time: 779 us; the launch traced here: 772 us
  other arithmetic  430 us (55%)
  blocking collectives  136 us (17%)
  starting transfers between devices  113 us (15%)
  waiting for transfers between devices  53.8 us (7%)
  local copies, waits for them, and re-layouts  22 us (3%)
  matrix products  15.7 us (2%)
    another operation x4, other arithmetic, shards(): factor = jnp.linalg.cholesky(coarse_matrix)  191 us
    another operation x3, other arithmetic, coarse_solve(): lax.linalg.triangular_solve(factor, forward, left_side=True, lower=True,...  160 us
    all_to_all x12, blocking collectives, from_everyone(): return lax.all_to_all(copies, axis, split_axis=0, concat_axis=0, tiled=True)  106 us
    all_to_all x6, starting transfers between devices, from_everyone(): return lax.all_to_all(copies, axis, split_axis=0, concat_axis=0, tiled=True)  39.7 us
    add x9, other arithmetic, smooth(): window(iterate, 1, height, breadth)  31.6 us
    all_gather x1, blocking collectives, rows_first(): out = lax.all_gather(both, axis, axis=0, tiled=True)  30.3 us
    ppermute x8, starting transfers between devices, padded_2(): lax.ppermute(lax.slice_in_dim(block, block.shape[dim] - width, None, axis...  25.2 us
    all_to_all x6, waiting for transfers between devices, from_everyone(): return lax.all_to_all(copies, axis, split_axis=0, concat_axis=0, tiled=True)  23.9 us
  transfers between devices with their start and end apart: 34, of which 19 were waited for; matrix products, arithmetic and copies ran while one was open for 51% of the time, Pallas kernels for 0%

commit v1 on v0

v1 whole, which is shorter than its diff:
```python
import jax
import jax.numpy as jnp
from jax import lax
from jax.experimental import pallas as pl
from jax.experimental.pallas import tpu as pltpu
from jax.sharding import PartitionSpec as P

LEAKAGE = 0.0001
RELAXATION = 2.0 / 3.0
NB = 16
CR = 32
CC = 512
N_ROW = 16
N_COL = 8
NC = N_COL * CC
MARGIN = 16
WR = CR + 2 * MARGIN
WC = CC + 128
F32 = jnp.float32
BF16 = jnp.bfloat16
MESH = pl.DeviceIdType.MESH
NT = (((1,), (1,)), ((), ()))


def iota(shape, dim):
    return lax.broadcasted_iota(jnp.int32, shape, dim)


def roll(x, shift):
    return pltpu.roll(x, shift % x.shape[-1], x.ndim - 1)


def flat_row(x):
    pick = (iota((16, 256), 1) % 16 == iota((16, 256), 0)).astype(F32)
    tiled = jnp.dot(x, pick, precision=lax.Precision.HIGHEST, preferred_element_type=F32)
    own = iota((16, 256), 1) // 16 == iota((16, 256), 0)
    return jnp.sum(jnp.where(own, tiled, 0.0), axis=0, keepdims=True)


def mat_mat(a, b):
    out = []
    for j in range(8):
        total = a[0] * b[j][0:1, :]
        for k in range(1, 8):
            total = total + a[k] * b[j][k : k + 1, :]
        out.append(total)
    return out


def mat_vec(a, f):
    parts = [a[k] * f[k : k + 1, :] for k in range(8)]
    while len(parts) > 1:
        parts = [parts[i] + parts[i + 1] for i in range(0, len(parts), 2)]
    return parts[0]


def mat_inv(t):
    t = list(t)
    sub = iota((8, 256), 0)
    for k in range(8):
        pivot = 1.0 / t[k][k : k + 1, :]
        column = t[k]
        at_k = sub == k
        for j in range(8):
            if j != k:
                row = t[j][k : k + 1, :] * pivot
                t[j] = jnp.where(at_k, row, t[j] - column * row)
        t[k] = jnp.where(at_k, pivot, -column * pivot)
    return t


def body(
    cond, mask, sidx, scur, gidx, out,
    mwin, side_r, side_l, diag, hsrc, winv, e_east, e_south, kappa,
    s_a, s_b, v0, v1, w0, w1, lhs_g, lhs_s, cfac, clow, cup, mrow,
    ga0, gb0, ga1, gb1, ga2, gb2, ga3, gb3,
    halo_send, halo_recv, ga_send, ga_recv, gb_send, gb_recv,
):
    rho = lax.axis_index("row")
    col = lax.axis_index("col")
    gas = (ga0, ga1, ga2, ga3)
    gbs = (gb0, gb1, gb2, gb3)

    barrier = pltpu.get_barrier_semaphore()
    for i in range(1, N_COL):
        pl.semaphore_signal(barrier, inc=1, device_id=(rho, lax.rem(col + i, N_COL)), device_id_type=MESH)
    for i in range(1, N_ROW):
        pl.semaphore_signal(barrier, inc=1, device_id=(lax.rem(rho + i, N_ROW), col), device_id_type=MESH)
    diagonals = ((-1, -1), (-1, 1), (1, -1), (1, 1))

    def exists(dr, dc):
        ok = None
        for at, step, size in ((rho, dr, N_ROW), (col, dc, N_COL)):
            if step:
                here = (at > 0) if step < 0 else (at < size - 1)
                ok = here if ok is None else jnp.logical_and(ok, here)
        return ok

    for dr, dc in diagonals:
        @pl.when(exists(dr, dc))
        def _():
            pl.semaphore_signal(barrier, inc=1, device_id=(rho + dr, col + dc), device_id_type=MESH)

    mwin[MARGIN : MARGIN + CR, 0:CC] = cond[...] * mask[...].astype(F32)

    def land(dr, dc):
        rows = {-1: pl.ds(0, MARGIN), 0: pl.ds(MARGIN, CR), 1: pl.ds(MARGIN + CR, MARGIN)}[dr]
        if dc == 0:
            return mwin.at[rows, pl.ds(0, CC)]
        return (side_r if dc > 0 else side_l).at[rows, :]

    def take(dr, dc):
        rows = {-1: pl.ds(MARGIN, MARGIN), 0: pl.ds(MARGIN, CR), 1: pl.ds(MARGIN + CR - MARGIN, MARGIN)}[dr]
        cols = {-1: pl.ds(0, 128), 0: pl.ds(0, CC), 1: pl.ds(CC - 128, 128)}[dc]
        return mwin.at[rows, cols]

    around = [(dr, dc) for dr in (-1, 0, 1) for dc in (-1, 0, 1) if dr or dc]
    for dr, dc in around:
        @pl.when(jnp.logical_not(exists(dr, dc)))
        def _():
            ref = land(dr, dc)
            ref[...] = jnp.zeros(ref.shape, F32)

    def halo_copy(n, dr, dc):
        m = around.index((-dr, -dc))
        return pltpu.make_async_remote_copy(
            src_ref=take(dr, dc), dst_ref=land(-dr, -dc),
            send_sem=halo_send.at[n], recv_sem=halo_recv.at[m],
            device_id=(rho + dr, col + dc), device_id_type=MESH,
        )

    gflat = flat_row(gidx[...].astype(F32)).astype(jnp.int32)
    sflat = flat_row(sidx[...].astype(F32)).astype(jnp.int32)
    cflat = flat_row(scur[...])
    g_row, g_col = gflat // NC, gflat % NC
    s_row, s_col = sflat // NC, sflat % NC

    expected = N_COL - 1 + N_ROW - 1
    for dr, dc in diagonals:
        expected = expected + exists(dr, dc).astype(jnp.int32)
    pl.semaphore_wait(barrier, expected)

    for n, (dr, dc) in enumerate(around):
        @pl.when(exists(dr, dc))
        def _():
            halo_copy(n, dr, dc).start()

    own_b = iota((NB, 256), 1) // 16 == iota((NB, 256), 0)
    g_rel = g_row - rho * CR + MARGIN
    s_rel = s_row - rho * CR + MARGIN
    c_hi = cflat.astype(BF16).astype(F32)
    c_mid = (cflat - c_hi).astype(BF16).astype(F32)
    c_lo = cflat - c_hi - c_mid

    def build(r, carry):
        g_hit = jnp.logical_and(own_b, g_rel == r)
        s_hit = jnp.logical_and(own_b, s_rel == r)
        lhs_g[r] = jnp.where(g_hit, 1.0, 0.0).astype(BF16)
        lhs_s[r, :, 0:256] = jnp.where(s_hit, c_hi, 0.0).astype(BF16)
        lhs_s[r, :, 256:512] = jnp.where(s_hit, c_mid, 0.0).astype(BF16)
        lhs_s[r, :, 512:768] = jnp.where(s_hit, c_lo, 0.0).astype(BF16)
        return carry

    lax.fori_loop(0, WR, build, 0)

    def place(column):
        rel = column - col * CC
        return jnp.where(rel >= 576, -1, jnp.where(rel >= 0, rel, jnp.where(rel >= -64, rel + WC, -1)))

    g_hot = jnp.where(place(g_col) == iota((WC, 256), 0), 1.0, 0.0).astype(BF16)
    s_one = jnp.where(place(s_col) == iota((WC, 256), 0), 1.0, 0.0).astype(BF16)
    s_hot = jnp.concatenate([s_one, s_one, s_one], axis=1)

    STEP = 16

    def spread(i, carry):
        rows = pl.ds(i * STEP, STEP)
        diag[rows] = lax.dot_general(
            lhs_g[rows].reshape(STEP * NB, 256), g_hot, NT, preferred_element_type=F32
        ).reshape(STEP, NB, WC)
        hsrc[rows] = lax.dot_general(
            lhs_s[rows].reshape(STEP * NB, 768), s_hot, NT, preferred_element_type=F32
        ).reshape(STEP, NB, WC)
        return carry

    lax.fori_loop(0, WR // STEP, spread, 0)

    a1 = jnp.where(g_col // CC == iota((8, 256), 0), 1.0, 0.0).astype(BF16)
    a2 = jnp.where(
        jnp.logical_and(
            g_row // CR == iota((256, 256), 0) // 16,
            iota((256, 256), 1) // 16 == iota((256, 256), 0) % 16,
        ), 1.0, 0.0).astype(BF16)
    shunt_total = lax.dot_general(a1, a2, NT, preferred_element_type=F32)

    for n, (dr, dc) in enumerate(around):
        @pl.when(exists(dr, dc))
        def _():
            halo_copy(n, dr, dc).wait_send()
            ref = land(dr, dc)
            pltpu.make_async_remote_copy(
                src_ref=ref, dst_ref=ref, send_sem=halo_send.at[n], recv_sem=halo_recv.at[n],
                device_id=(rho + dr, col + dc), device_id_type=MESH,
            ).wait_recv()
    lane = iota((WR, 128), 1)
    mwin[0:WR, CC:WC] = jnp.where(lane < 64, side_r[...], side_l[...])
    mwin[WR : WR + 8, :] = jnp.zeros((8, WC), F32)

    m = mwin[0:WR, :]
    m_s = mwin[1 : WR + 1, :]
    present = jnp.where(m > 0.0, 1.0, 0.0)
    present_s = jnp.where(m_s > 0.0, 1.0, 0.0)
    east = 0.5 * present * roll(present, -1) * (m + roll(m, -1))
    south = 0.5 * present * present_s * (m + m_s)
    west = roll(east, 1)
    mrow[0] = south
    north = jnp.concatenate([jnp.zeros((1, WC), F32), mrow[0, 0 : WR - 1, :]], axis=0)
    base = east + west + south + north + LEAKAGE
    mrow[1] = base
    mrow[2] = east
    mrow[3] = present
    at_r = iota((WR, WC), 0)
    at_c = iota((WR, WC), 1)
    row_in = jnp.where(jnp.logical_and(at_r >= MARGIN, at_r < MARGIN + CR), 1.0, 0.0)
    row_in_s = jnp.where(jnp.logical_and(at_r >= MARGIN - 1, at_r < MARGIN + CR - 1), 1.0, 0.0)
    row_in_n = jnp.where(jnp.logical_and(at_r >= MARGIN + 1, at_r < MARGIN + CR + 1), 1.0, 0.0)
    col_in = jnp.where(at_c < CC, 1.0, 0.0)
    col_in_e = jnp.where(jnp.logical_or(at_c < CC - 1, at_c == WC - 1), 1.0, 0.0)
    col_in_w = jnp.where(jnp.logical_and(at_c >= 1, at_c <= CC), 1.0, 0.0)
    inside = row_in * col_in
    mrow[4] = (
        base * inside - east * (row_in * col_in_e) - west * (row_in * col_in_w)
        - south * (row_in_s * col_in) - north * (row_in_n * col_in)
    )
    gap_field = ((((base - east) - west) - south) - north - LEAKAGE) * inside
    east_field = jnp.where(at_c == CC - 1, east * row_in, 0.0)
    south_field = jnp.where(at_r == MARGIN + CR - 1, south * col_in, 0.0)

    def total(field):
        return jnp.sum(jnp.sum(field, axis=0, keepdims=True), axis=1, keepdims=True)

    slot = iota((NB, 128), 1) // 16
    own_slot = slot == lax.rem(rho, 8)
    same_b = iota((NB, 128), 1) % 16 == iota((NB, 128), 0)
    row_slot = iota((1, 128), 1) // 16 == lax.rem(rho, 8)

    def one_row(value):
        return jnp.where(row_slot, jnp.broadcast_to(value, (1, 128)), 0.0)

    def b_row(acc, where):
        value = jnp.sum(acc, axis=1, keepdims=True)
        return jnp.sum(jnp.where(jnp.logical_and(where, same_b), value, 0.0), axis=0, keepdims=True)

    def fold(x):
        parts = [x[:, 128 * i : 128 * (i + 1)] for i in range(x.shape[1] // 128)]
        acc = parts[0]
        for p in parts[1:]:
            acc = acc + p
        return acc

    def send_a(g, rows):
        ga = gas[g]
        ga[col] = jnp.concatenate(rows, axis=0)
        for i in range(1, N_COL):
            pltpu.make_async_remote_copy(
                src_ref=ga.at[col], dst_ref=ga.at[col], send_sem=ga_send.at[g], recv_sem=ga_recv.at[g],
                device_id=(rho, lax.rem(col + i, N_COL)), device_id_type=MESH,
            ).start()

    def send_b(g):
        ga, gb = gas[g], gbs[g]
        peers = pl.ds(0, N_COL - 1)
        pltpu.make_async_remote_copy(
            src_ref=ga.at[peers], dst_ref=ga.at[peers], send_sem=ga_send.at[g], recv_sem=ga_recv.at[g],
            device_id=(rho, lax.rem(col + 1, N_COL)), device_id_type=MESH,
        ).wait()
        for i in range(1, N_ROW):
            pltpu.make_async_remote_copy(
                src_ref=ga, dst_ref=gb.at[rho], send_sem=gb_send.at[g], recv_sem=gb_recv.at[g],
                device_id=(lax.rem(rho + i, N_ROW), col), device_id_type=MESH,
            ).start()
        gb[rho] = ga[...]

    def wait_b(g):
        gb = gbs[g]
        peers = pl.ds(0, N_ROW - 1)
        pltpu.make_async_remote_copy(
            src_ref=gb.at[peers], dst_ref=gb.at[peers], send_sem=gb_send.at[g], recv_sem=gb_recv.at[g],
            device_id=(lax.rem(rho + 1, N_ROW), col), device_id_type=MESH,
        ).wait()

    def coarse(g, k):
        gb = gbs[g]
        halves = []
        for h in range(2):
            acc = gb[8 * h, :, k, :]
            for i in range(1, 8):
                acc = acc + gb[8 * h + i, :, k, :]
            halves.append(acc)
        return jnp.concatenate(halves, axis=1)

    def mask_rows(r, carry):
        here = hsrc[r] * mrow[3, pl.ds(r, 1), :]
        hsrc[r] = here
        return carry

    lax.fori_loop(0, WR, mask_rows, 0, unroll=4)

    def sum_rows(r, acc):
        return acc + fold(hsrc[r, :, 0:CC])

    inflow_acc = lax.fori_loop(MARGIN, MARGIN + CR, sum_rows, jnp.zeros((NB, 128), F32), unroll=4)
    send_a(0, [
        b_row(inflow_acc, own_slot), one_row(total(east_field)), one_row(total(south_field)), one_row(total(gap_field)),
    ])

    def coeffs(r, carry):
        rows = pl.ds(r, 1)
        d = diag[r] + mrow[1, rows, :]
        inverse = RELAXATION / d
        winv[r] = inverse
        s_a[r] = inverse * hsrc[r]
        e_east[r] = jnp.broadcast_to(mrow[2, rows, :], (8, WC))
        e_south[r] = jnp.broadcast_to(mrow[0, rows, :], (8, WC))
        kappa[r] = jnp.broadcast_to(mrow[4, rows, :], (8, WC))
        return carry

    lax.fori_loop(0, WR, coeffs, 0, unroll=2)

    def sweep(src, dst, width, extra=None, image=None):
        def cell(r, half, acc):
            sub = pl.ds(8 * half, 8)
            s = src[r, sub, :]
            e = e_east[r]
            t = e * roll(s, -1) + roll(e * s, 1)
            t = t + e_south[r] * src[r + 1, sub, :] + e_south[r - 1] * src[r - 1, sub, :]
            if dst is not None:
                new = s * (1.0 / 3.0) + winv[r, sub, :] * t
                if extra is not None:
                    new = new + extra[r, sub, :]
                dst[r, sub, :] = new
            if acc is not None:
                si = s[:, 0:CC]
                d = diag[r, sub, 0:CC] + mrow[1, pl.ds(r, 1), 0:CC]
                w = d * si - t[:, 0:CC]
                ref, dots = image
                if ref is not None:
                    ref[r - MARGIN, sub, :] = w
                acc = tuple(
                    a + fold((si if f is None else f[r - (0 if f.shape[0] == WR else MARGIN), sub, 0:CC]) * (w if h is None else h[r - MARGIN, sub, :]))
                    for a, (f, h) in zip(acc, dots)
                )
            return acc

        def plain(r, carry):
            cell(r, 0, None)
            cell(r, 1, None)
            return carry

        lo, hi = MARGIN - width, MARGIN + CR + width
        if image is None:
            lax.fori_loop(0, (hi - lo) // 2, lambda i, c: plain(lo + 2 * i + 1, plain(lo + 2 * i, c)), 0)
            return None
        if lo < MARGIN:
            lax.fori_loop(lo, MARGIN, plain, 0)
            lax.fori_loop(MARGIN + CR, hi, plain, 0)
        zero = tuple(jnp.zeros((8, 128), F32) for _ in image[1])

        def rich(r, carry):
            return cell(r, 0, carry[0]), cell(r, 1, carry[1])

        top, bottom = lax.fori_loop(MARGIN, MARGIN + CR, rich, (zero, zero))
        return [jnp.concatenate([a, b], axis=0) for a, b in zip(top, bottom)]

    def block_image(field, also=None):
        def step(r, carry):
            acc, acc2 = carry
            f = field[r]
            k = kappa[r]
            acc = acc + fold(f * jnp.concatenate([k, k], axis=0))
            return acc, acc2

        def inner(r, carry):
            acc, acc2 = step(r, carry)
            fi = field[r, :, 0:CC]
            acc = acc + fold(fi * diag[r, :, 0:CC])
            if also is not None:
                acc2 = acc2 + fold(fi * also[r, :, 0:CC])
            return acc, acc2

        zero = jnp.zeros((NB, 128), F32)
        carry = step(MARGIN - 1, (zero, zero))
        carry = lax.fori_loop(MARGIN, MARGIN + CR, inner, carry, unroll=2)
        return step(MARGIN + CR, carry)

    def keep(r, carry):
        v1[r] = s_a[r]
        return carry

    lax.fori_loop(0, WR, keep, 0, unroll=2)
    sweep(v1, s_a, 14, extra=v1)
    sweep(s_a, s_b, 13, extra=v1)
    send_b(0)
    sweep(s_b, s_a, 12, extra=v1)
    sweep(s_a, s_b, 11, extra=v1)
    ra, ru = block_image(s_b, hsrc)
    zero_row = jnp.zeros((1, 128), F32)
    send_a(1, [b_row(ra, own_slot), zero_row])

    wait_b(0)
    f0 = coarse(0, 0)
    ec = coarse(0, 1)
    sc = coarse(0, 2)
    gap = coarse(0, 3)
    degree = LEAKAGE * CR * CC + shunt_total + ec + pltpu.roll(ec, 1, 0) + sc + roll(sc, 16)
    sub = iota((8, 256), 0)
    t = []
    for j in range(8):
        tj = jnp.where(sub == j, degree, 0.0)
        tj = jnp.where(sub == j - 1, -ec, tj)
        tj = jnp.where(sub == j + 1, -jnp.broadcast_to(ec[j : j + 1, :], (8, 256)), tj)
        t.append(tj)
    uvec = -sc
    lvec = roll(uvec, 16)
    x = mat_inv(t)
    for j in range(8):
        cfac[0, j] = x[j]
    ux = [uvec * x[j] for j in range(8)]
    lx = [lvec * x[j] for j in range(8)]
    p = [ux[j] * uvec[j : j + 1, :] for j in range(8)]
    q = [lx[j] * lvec[j : j + 1, :] for j in range(8)]
    w = [ux[j] * lvec[j : j + 1, :] for j in range(8)]
    wt = [lx[j] * uvec[j : j + 1, :] for j in range(8)]
    for level in range(1, 5):
        d = 16 << (level - 1)
        t = [t[j] - roll(p[j], d) - roll(q[j], -d) for j in range(8)]
        x = mat_inv(t)
        for j in range(8):
            cfac[level, j] = x[j]
        if level == 4:
            break
        low = [-roll(w[j], d) for j in range(8)]
        up = [-roll(wt[j], -d) for j in range(8)]
        low_t = [-roll(wt[j], d) for j in range(8)]
        up_t = [-roll(w[j], -d) for j in range(8)]
        for j in range(8):
            clow[level - 1, j] = low[j]
            cup[level - 1, j] = up[j]
        y = mat_mat(x, up)
        z = mat_mat(x, low)
        p = mat_mat(up_t, y)
        q = mat_mat(low_t, z)
        w = mat_mat(up_t, z)
        wt = mat_mat(low_t, y)

    def solve(f):
        h = mat_vec([cfac[0, j] for j in range(8)], f)
        f = f - lvec * roll(h, 16) - uvec * roll(h, -16)
        for level in range(1, 4):
            d = 16 << level
            h = mat_vec([cfac[level, j] for j in range(8)], f)
            f = f - mat_vec([clow[level - 1, j] for j in range(8)], roll(h, d))
            f = f - mat_vec([cup[level - 1, j] for j in range(8)], roll(h, -d))
        return mat_vec([cfac[4, j] for j in range(8)], f)

    wide_b = iota((NB, 256), 1) % 16 == iota((NB, 256), 0)

    def to_b(row):
        return jnp.sum(jnp.where(wide_b, row, 0.0), axis=1, keepdims=True)

    def dot_c(a, b):
        return to_b(jnp.sum(a * b, axis=0, keepdims=True))

    lane_c = iota((NB, WC), 1)

    def around_field(y):
        fields = []
        lane_row = iota((8, 256), 1) // 16
        for dr in (-1, 0, 1):
            vals = []
            for dc in (0, 1, -1):
                hit = jnp.logical_and(lane_row == rho + dr, sub == col + dc)
                vals.append(to_b(jnp.sum(jnp.where(hit, y, 0.0), axis=0, keepdims=True)))
            fields.append(jnp.where(lane_c < CC, vals[0], jnp.where(lane_c < CC + 64, vals[1], vals[2])))
        return fields

    def combine(dst, src, fields, width, sign):
        spans = ((MARGIN - width, MARGIN), (MARGIN, MARGIN + CR), (MARGIN + CR, MARGIN + CR + width))
        for (lo, hi), field in zip(spans, fields):
            def step(r, carry):
                dst[r] = field + src[r] if sign > 0 else field - src[r]
                return carry
            lax.fori_loop(lo, hi, step, 0)

    y0 = solve(f0)
    send_b(1)
    combine(v0, s_b, around_field(y0), 11, 1)

    (mu0,) = sweep(v0, s_a, 10, image=(w0, ((None, None),)))
    sweep(s_a, s_b, 9)
    sweep(s_b, s_a, 8)
    sweep(s_a, s_b, 7)
    sweep(s_b, s_a, 6)
    ra0, _ = block_image(s_a)
    send_a(2, [b_row(ra0, own_slot), zero_row])
    wait_b(1)
    f1 = f0 + coarse(1, 0) + gap * y0
    g0 = solve(f1)
    combine(v1, s_a, around_field(g0), 6, -1)

    mu2, mu1 = sweep(v1, s_b, 5, image=(w1, ((None, None), (None, w0))))
    sweep(s_b, s_a, 4)
    sweep(s_a, s_b, 3)
    send_b(2)
    sweep(s_b, s_a, 2)
    sweep(s_a, s_b, 1)
    bab, bw1 = sweep(s_b, None, 0, image=(None, ((None, None), (None, w1))))
    ra1, _ = block_image(s_b)
    moments = zero_row
    for n, acc in enumerate((ru, mu0, mu1, mu2, bw1, bab)):
        moments = moments + b_row(acc, slot == n)
    send_a(3, [b_row(ra1, own_slot), moments])
    wait_b(2)
    f2 = f1 - coarse(2, 0) + gap * g0
    g1 = solve(f2)
    energy_y = dot_c(f0, y0)
    g1w1 = dot_c(g1, f2)
    g1gap = dot_c(g1, g1 * gap)
    send_b(3)
    wait_b(3)
    ra1_all = coarse(3, 0)
    g1ra1 = dot_c(g1, ra1_all)
    mom = coarse(3, 1)
    mom = jnp.sum(mom[:, 0:128] + mom[:, 128:256], axis=0, keepdims=True)

    def moment(n):
        return jnp.sum(jnp.where(jnp.logical_and(slot == n, same_b), mom, 0.0), axis=1, keepdims=True)

    energy = moment(0) + energy_y
    m0, m1, m2 = moment(1), moment(2), moment(3)
    m3 = g1w1 - moment(4)
    m4 = g1w1 + g1gap - 2.0 * g1ra1 + moment(5)
    r1 = m0 - energy
    r2 = m1 - r1

    def ratio(a, b, scale):
        ok = b > scale
        return jnp.where(ok, a / jnp.where(ok, b, 1.0), 0.0)

    l10 = m1 / m0
    l20 = m2 / m0
    d1 = m2 - l10 * m1
    e21 = m3 - l20 * m1
    l21 = ratio(e21, d1, 0.0)
    d2 = m4 - l20 * m2 - l21 * e21
    t1 = r1 - l10 * energy
    t2 = r2 - l20 * energy - l21 * t1
    c2 = ratio(t2, d2, 0.0)
    c1 = ratio(t1, d1, 0.0) - l21 * c2
    c0 = energy / m0 - l10 * c1 - l20 * c2
    hit = jnp.logical_and(iota((8, 256), 1) // 16 == rho, sub == col)
    shift = c2 * to_b(jnp.sum(jnp.where(hit, g1, 0.0), axis=0, keepdims=True))
    c0 = jnp.broadcast_to(c0, (NB, CC))
    c1 = jnp.broadcast_to(c1, (NB, CC))
    c2 = jnp.broadcast_to(c2, (NB, CC))
    shift = jnp.broadcast_to(shift, (NB, CC))

    def finish(r, carry):
        w = r + MARGIN
        out[r] = c0 * v0[w, :, 0:CC] + c1 * v1[w, :, 0:CC] - c2 * s_b[w, :, 0:CC] + shift
        return carry

    lax.fori_loop(0, CR, finish, 0, unroll=2)


def shards(conductance, nodata_mask, source_index, source_current, ground_index):
    big = pltpu.VMEM((WR, NB, WC), F32)
    edge = pltpu.VMEM((WR, 8, WC), F32)
    own = pltpu.VMEM((CR, NB, CC), F32)
    scratch = [
        pltpu.VMEM((WR + 8, WC), F32), pltpu.VMEM((WR, 128), F32), pltpu.VMEM((WR, 128), F32),
        big, big, big, edge, edge, edge,
        big, big, big, big, own, own,
        pltpu.VMEM((WR, NB, 256), BF16), pltpu.VMEM((WR, NB, 768), BF16),
        pltpu.VMEM((5, 8, 8, 256), F32), pltpu.VMEM((3, 8, 8, 256), F32), pltpu.VMEM((3, 8, 8, 256), F32),
        pltpu.VMEM((5, WR, WC), F32),
    ]
    for q in (4, 2, 2, 2):
        scratch += [pltpu.VMEM((N_COL, q, 128), F32), pltpu.VMEM((N_ROW, N_COL, q, 128), F32)]
    scratch += [pltpu.SemaphoreType.DMA((8,)), pltpu.SemaphoreType.DMA((8,))]
    scratch += [pltpu.SemaphoreType.DMA((4,)) for _ in range(4)]
    voltage = pl.pallas_call(
        body,
        out_shape=jax.ShapeDtypeStruct((CR, NB, CC), F32),
        in_specs=[pl.BlockSpec(memory_space=pltpu.VMEM)] * 5,
        out_specs=pl.BlockSpec(memory_space=pltpu.VMEM),
        scratch_shapes=scratch,
        compiler_params=pltpu.CompilerParams(
            collective_id=0, has_side_effects=True, vmem_limit_bytes=56 * 1024 * 1024
        ),
    )(conductance, nodata_mask, source_index, source_current, ground_index)
    return jnp.transpose(voltage, (1, 0, 2))


def solution(mesh):
    return jax.shard_map(
        shards,
        mesh=mesh,
        in_specs=(P("row", "col"), P("row", "col"), P(), P(), P()),
        out_specs=P(None, "row", "col"),
        check_vma=False,
    )
```

time: 779 us -> 80.1 us (0.10)
  other arithmetic: 430 us -> 0 us
  blocking collectives: 136 us -> 0 us
  starting transfers between devices: 113 us -> 0 us
  Pallas kernels: 0 us -> 77 us
  waiting for transfers between devices: 53.8 us -> 0 us
  local copies, waits for them, and re-layouts: 22 us -> 2.81 us
  matrix products: 15.7 us -> 0 us
    another operation x8 -> x0, other arithmetic: 351 us -> none  [the longest x4 191 us: shards(): factor = jnp.linalg.cholesky(coarse_matrix)]
    all_to_all x12 -> x0, blocking collectives: 106 us -> none  [from_everyone(): return lax.all_to_all(copies, axis, split_axis=0, concat_axis=0, tiled=True)]
    pallas_call x0 -> x1, Pallas kernels: none -> 77 us  [shards(): pl.pallas_call(body, out_shape=jax.ShapeDtypeStruct((CR, NB, CC), F32), i...]
    ppermute x28 -> x0, starting transfers between devices: 73 us -> none  [the longest x8 25.2 us: padded_2(): lax.ppermute(lax.slice_in_dim(block, block.shape[dim] - width, None, axis...]
    add x20 -> x0, other arithmetic: 40.3 us -> none  [the longest x9 31.6 us: smooth(): window(iterate, 1, height, breadth)]
    all_to_all x6 -> x0, starting transfers between devices: 39.7 us -> none  [from_everyone(): return lax.all_to_all(copies, axis, split_axis=0, concat_axis=0, tiled=True)]
    all_gather x1 -> x0, blocking collectives: 30.3 us -> none  [rows_first(): out = lax.all_gather(both, axis, axis=0, tiled=True)]
    ppermute x28 -> x0, waiting for transfers between devices: 29.9 us -> none  [the longest x8 16.5 us: padded_2(): lax.ppermute(lax.slice_in_dim(block, 0, width, axis=dim), axis, backward)]
  transfers between devices with their start and end apart: 34 -> 0, of which waited for: 19 -> 0; matrix products, arithmetic and copies ran while one was open for 51% -> 0% of each run, Pallas kernels for 0% -> 0%
where the time goes in v1:
time: 80.1 us; the launch traced here: 79.9 us
  Pallas kernels  77 us (96%)
  local copies, waits for them, and re-layouts  2.81 us (4%)
    pallas_call x1, Pallas kernels, shards(): pl.pallas_call(body, out_shape=jax.ShapeDtypeStruct((CR, NB, CC), F32), i...  77 us
    transpose x1, local copies, waits for them, and re-layouts, shards(): return jnp.transpose(voltage, (1, 0, 2))  2.81 us

profile of v1, /device:TPU:1, one launch (start us, length us, event | category | flops | bytes accessed | tf_op | source)
XLA Modules:
  0.0 79.9 jit_solution(1681731229916317427)
XLA Ops:
  0.0 77.0 %shard_map.55 = f32[32,16,512]{2,1,0:T(8,128)} custom-call(f32[32,512]{1,0:T(8,128)} %cond.1, s32[32,512]{1,0:T(8,128)} %mask.1, s32[16,16]{1,0:T(8,128)} %sidx.1, f32[16,16]{1,0:T(8,128)} %scur.1, s32[16,16]{1,0:T(8,128)} %gidx.1), custom_call_target="tpu_custom_call" | custom-call | tf_op jit(solution)/shard_map/pallas_call | solution.py:592
  77.0 2.8 %copy.6 = f32[16,32,512]{2,1,0:T(8,128)} copy(f32[16,32,512]{2,0,1:T(8,128)} %bitcast.1) | data formatting | bytes 2097152 | tf_op jit(solution)/shard_map/transpose | solution.py:602

commit v2 on v1

--- a/solution.py
+++ b/solution.py
@@ -14,6 +14,7 @@
 N_COL = 8
 NC = N_COL * CC
 MARGIN = 16
+STEP_ROWS = 6
 WR = CR + 2 * MARGIN
 WC = CC + 128
 F32 = jnp.float32
@@ -28,6 +29,56 @@
 
 def roll(x, shift):
     return pltpu.roll(x, shift % x.shape[-1], x.ndim - 1)
+
+
+def at_col():
+    c = iota((1, WC), 1)
+    return 5 * (c % 128) + c // 128
+
+
+def tiles(x):
+    return [x[..., 128 * j : 128 * (j + 1)] for j in range(WC // 128)]
+
+
+def east_of(x):
+    t = tiles(x)
+    return jnp.concatenate(t[1:] + [roll(t[0], -1)], axis=-1)
+
+
+def west_of(x):
+    t = tiles(x)
+    return jnp.concatenate([roll(t[-1], 1)] + t[:-1], axis=-1)
+
+
+def interleave(x):
+    n = x.shape[0]
+    lane = iota((n, 128), 1)
+    source = tiles(x)
+    out = []
+    for j in range(5):
+        p = 5 * lane + j
+        part = None
+        for t in range(5):
+            got = jnp.take_along_axis(source[t], p % 128, axis=1)
+            part = got if part is None else jnp.where(p // 128 == t, got, part)
+        out.append(part)
+    return jnp.concatenate(out, axis=1)
+
+
+def natural(parts):
+    n = parts[0].shape[0]
+    lane = iota((n, 128), 1)
+    out = []
+    for t in range(CC // 128):
+        c = 128 * t + lane
+        fifth = (c * 52429) >> 18
+        j_of = c - 5 * fifth
+        tile = None
+        for j in range(5):
+            got = jnp.take_along_axis(parts[j], fifth, axis=1)
+            tile = got if tile is None else jnp.where(j_of == j, got, tile)
+        out.append(tile)
+    return jnp.concatenate(out, axis=1)
 
 
 def flat_row(x):
@@ -71,10 +122,10 @@
 
 def body(
     cond, mask, sidx, scur, gidx, out,
-    mwin, side_r, side_l, diag, hsrc, winv, e_east, e_south, kappa,
+    mwin, side_r, side_l, diag, hsrc, winv3, e_east, e_south, kappa,
     s_a, s_b, v0, v1, w0, w1, lhs_g, lhs_s, cfac, clow, cup, mrow,
     ga0, gb0, ga1, gb1, ga2, gb2, ga3, gb3,
-    halo_send, halo_recv, ga_send, ga_recv, gb_send, gb_recv,
+    nat, coef, halo_send, halo_recv, ga_send, ga_recv, gb_send, gb_recv,
 ):
     rho = lax.axis_index("row")
     col = lax.axis_index("col")
@@ -167,8 +218,9 @@
         rel = column - col * CC
         return jnp.where(rel >= 576, -1, jnp.where(rel >= 0, rel, jnp.where(rel >= -64, rel + WC, -1)))
 
-    g_hot = jnp.where(place(g_col) == iota((WC, 256), 0), 1.0, 0.0).astype(BF16)
-    s_one = jnp.where(place(s_col) == iota((WC, 256), 0), 1.0, 0.0).astype(BF16)
+    spot = 5 * (iota((WC, 256), 0) % 128) + iota((WC, 256), 0) // 128
+    g_hot = jnp.where(place(g_col) == spot, 1.0, 0.0).astype(BF16)
+    s_one = jnp.where(place(s_col) == spot, 1.0, 0.0).astype(BF16)
     s_hot = jnp.concatenate([s_one, s_one, s_one], axis=1)
 
     STEP = 16
@@ -204,23 +256,24 @@
             ).wait_recv()
     lane = iota((WR, 128), 1)
     mwin[0:WR, CC:WC] = jnp.where(lane < 64, side_r[...], side_l[...])
-    mwin[WR : WR + 8, :] = jnp.zeros((8, WC), F32)
-
-    m = mwin[0:WR, :]
-    m_s = mwin[1 : WR + 1, :]
+
+    m = interleave(mwin[...])
+    mrow[0] = m
+    last = jnp.zeros((1, WC), F32)
+    m_s = jnp.concatenate([mrow[0, 1:WR, :], last], axis=0)
     present = jnp.where(m > 0.0, 1.0, 0.0)
     present_s = jnp.where(m_s > 0.0, 1.0, 0.0)
-    east = 0.5 * present * roll(present, -1) * (m + roll(m, -1))
+    east = 0.5 * present * east_of(present) * (m + east_of(m))
     south = 0.5 * present * present_s * (m + m_s)
-    west = roll(east, 1)
+    west = west_of(east)
     mrow[0] = south
-    north = jnp.concatenate([jnp.zeros((1, WC), F32), mrow[0, 0 : WR - 1, :]], axis=0)
+    north = jnp.concatenate([last, mrow[0, 0 : WR - 1, :]], axis=0)
     base = east + west + south + north + LEAKAGE
     mrow[1] = base
     mrow[2] = east
     mrow[3] = present
     at_r = iota((WR, WC), 0)
-    at_c = iota((WR, WC), 1)
+    at_c = jnp.broadcast_to(at_col(), (WR, WC))
     row_in = jnp.where(jnp.logical_and(at_r >= MARGIN, at_r < MARGIN + CR), 1.0, 0.0)
     row_in_s = jnp.where(jnp.logical_and(at_r >= MARGIN - 1, at_r < MARGIN + CR - 1), 1.0, 0.0)
     row_in_n = jnp.where(jnp.logical_and(at_r >= MARGIN + 1, at_r < MARGIN + CR + 1), 1.0, 0.0)
@@ -232,6 +285,7 @@
         base * inside - east * (row_in * col_in_e) - west * (row_in * col_in_w)
         - south * (row_in_s * col_in) - north * (row_in_n * col_in)
     )
+    mrow[5] = inside
     gap_field = ((((base - east) - west) - south) - north - LEAKAGE) * inside
     east_field = jnp.where(at_c == CC - 1, east * row_in, 0.0)
     south_field = jnp.where(at_r == MARGIN + CR - 1, south * col_in, 0.0)
@@ -251,161 +305,144 @@
         value = jnp.sum(acc, axis=1, keepdims=True)
         return jnp.sum(jnp.where(jnp.logical_and(where, same_b), value, 0.0), axis=0, keepdims=True)
 
+    own_col = at_col() < CC
+
     def fold(x):
-        parts = [x[:, 128 * i : 128 * (i + 1)] for i in range(x.shape[1] // 128)]
-        acc = parts[0]
-        for p in parts[1:]:
-            acc = acc + p
-        return acc
+        parts = tiles(jnp.where(own_col, x, 0.0))
+        return parts[0] + parts[1] + ((parts[2] + parts[3]) + parts[4])
+
+    def put_natural(n, field, lo, hi):
+        def step(r, carry):
+            for half in range(2):
+                sub = pl.ds(8 * half, 8)
+                nat[n, sub, r, :] = natural(tiles(field[r + MARGIN, sub, :]))
+            return carry
+
+        lax.fori_loop(lo, hi, step, 0, unroll=4)
 
     def send_a(g, rows):
         ga = gas[g]
-        ga[col] = jnp.concatenate(rows, axis=0)
+        ga[rho] = jnp.concatenate(rows, axis=0)
+        for i in range(1, N_ROW):
+            pltpu.make_async_remote_copy(
+                src_ref=ga.at[rho], dst_ref=ga.at[rho], send_sem=ga_send.at[g], recv_sem=ga_recv.at[g],
+                device_id=(lax.rem(rho + i, N_ROW), col), device_id_type=MESH,
+            ).start()
+
+    def send_b(g):
+        ga, gb = gas[g], gbs[g]
+        peers = pl.ds(0, N_ROW - 1)
+        pltpu.make_async_remote_copy(
+            src_ref=ga.at[peers], dst_ref=ga.at[peers], send_sem=ga_send.at[g], recv_sem=ga_recv.at[g],
+            device_id=(lax.rem(rho + 1, N_ROW), col), device_id_type=MESH,
+        ).wait()
+        for h in range(2):
+            acc = ga[8 * h]
+            for i in range(1, 8):
+                acc = acc + ga[8 * h + i]
+            gb[col, h] = acc
         for i in range(1, N_COL):
             pltpu.make_async_remote_copy(
-                src_ref=ga.at[col], dst_ref=ga.at[col], send_sem=ga_send.at[g], recv_sem=ga_recv.at[g],
+                src_ref=gb.at[col], dst_ref=gb.at[col], send_sem=gb_send.at[g], recv_sem=gb_recv.at[g],
                 device_id=(rho, lax.rem(col + i, N_COL)), device_id_type=MESH,
             ).start()
 
-    def send_b(g):
-        ga, gb = gas[g], gbs[g]
+    def wait_b(g):
+        gb = gbs[g]
         peers = pl.ds(0, N_COL - 1)
         pltpu.make_async_remote_copy(
-            src_ref=ga.at[peers], dst_ref=ga.at[peers], send_sem=ga_send.at[g], recv_sem=ga_recv.at[g],
+            src_ref=gb.at[peers], dst_ref=gb.at[peers], send_sem=gb_send.at[g], recv_sem=gb_recv.at[g],
             device_id=(rho, lax.rem(col + 1, N_COL)), device_id_type=MESH,
         ).wait()
-        for i in range(1, N_ROW):
-            pltpu.make_async_remote_copy(
-                src_ref=ga, dst_ref=gb.at[rho], send_sem=gb_send.at[g], recv_sem=gb_recv.at[g],
-                device_id=(lax.rem(rho + i, N_ROW), col), device_id_type=MESH,
-            ).start()
-        gb[rho] = ga[...]
-
-    def wait_b(g):
-        gb = gbs[g]
-        peers = pl.ds(0, N_ROW - 1)
-        pltpu.make_async_remote_copy(
-            src_ref=gb.at[peers], dst_ref=gb.at[peers], send_sem=gb_send.at[g], recv_sem=gb_recv.at[g],
-            device_id=(lax.rem(rho + 1, N_ROW), col), device_id_type=MESH,
-        ).wait()
 
     def coarse(g, k):
         gb = gbs[g]
-        halves = []
-        for h in range(2):
-            acc = gb[8 * h, :, k, :]
-            for i in range(1, 8):
-                acc = acc + gb[8 * h + i, :, k, :]
-            halves.append(acc)
-        return jnp.concatenate(halves, axis=1)
+        return jnp.concatenate([gb[:, 0, k, :], gb[:, 1, k, :]], axis=1)
 
     def mask_rows(r, carry):
         here = hsrc[r] * mrow[3, pl.ds(r, 1), :]
         hsrc[r] = here
-        return carry
-
-    lax.fori_loop(0, WR, mask_rows, 0, unroll=4)
-
-    def sum_rows(r, acc):
-        return acc + fold(hsrc[r, :, 0:CC])
-
-    inflow_acc = lax.fori_loop(MARGIN, MARGIN + CR, sum_rows, jnp.zeros((NB, 128), F32), unroll=4)
+        return carry + here * mrow[5, pl.ds(r, 1), :]
+
+    wide_zero = jnp.zeros((NB, WC), F32)
+    inflow_acc = lax.fori_loop(0, WR, mask_rows, wide_zero, unroll=4)
     send_a(0, [
-        b_row(inflow_acc, own_slot), one_row(total(east_field)), one_row(total(south_field)), one_row(total(gap_field)),
+        b_row(fold(inflow_acc), own_slot), one_row(total(east_field)), one_row(total(south_field)), one_row(total(gap_field)),
     ])
 
     def coeffs(r, carry):
         rows = pl.ds(r, 1)
-        d = diag[r] + mrow[1, rows, :]
-        inverse = RELAXATION / d
-        winv[r] = inverse
-        s_a[r] = inverse * hsrc[r]
+        shunt = diag[r]
+        d = shunt + mrow[1, rows, :]
+        inverse = 2.0 / d
+        diag[r] = d
+        winv3[r] = inverse
+        kappa[r] = mrow[4, rows, :] + shunt * mrow[5, rows, :]
+        v1[r] = (1.0 / 3.0) * inverse * hsrc[r]
         e_east[r] = jnp.broadcast_to(mrow[2, rows, :], (8, WC))
         e_south[r] = jnp.broadcast_to(mrow[0, rows, :], (8, WC))
-        kappa[r] = jnp.broadcast_to(mrow[4, rows, :], (8, WC))
         return carry
 
     lax.fori_loop(0, WR, coeffs, 0, unroll=2)
 
-    def sweep(src, dst, width, extra=None, image=None):
-        def cell(r, half, acc):
-            sub = pl.ds(8 * half, 8)
-            s = src[r, sub, :]
-            e = e_east[r]
-            t = e * roll(s, -1) + roll(e * s, 1)
-            t = t + e_south[r] * src[r + 1, sub, :] + e_south[r - 1] * src[r - 1, sub, :]
-            if dst is not None:
-                new = s * (1.0 / 3.0) + winv[r, sub, :] * t
-                if extra is not None:
-                    new = new + extra[r, sub, :]
-                dst[r, sub, :] = new
-            if acc is not None:
-                si = s[:, 0:CC]
-                d = diag[r, sub, 0:CC] + mrow[1, pl.ds(r, 1), 0:CC]
-                w = d * si - t[:, 0:CC]
-                ref, dots = image
-                if ref is not None:
-                    ref[r - MARGIN, sub, :] = w
-                acc = tuple(
-                    a + fold((si if f is None else f[r - (0 if f.shape[0] == WR else MARGIN), sub, 0:CC]) * (w if h is None else h[r - MARGIN, sub, :]))
-                    for a, (f, h) in zip(acc, dots)
-                )
-            return acc
-
-        def plain(r, carry):
-            cell(r, 0, None)
-            cell(r, 1, None)
+    def sweep(src, dst, width, extra=None, scale=None, image=None):
+        count = -(-(CR + 2 * width) // STEP_ROWS)
+        lo = MARGIN - width - (count * STEP_ROWS - CR - 2 * width) // 2
+
+        def step(i, carry):
+            r0 = lo + i * STEP_ROWS
+            for k in range(STEP_ROWS):
+                r = r0 + k
+                e = tiles(e_east[r])
+                south_here = tiles(e_south[r])
+                south_north = tiles(e_south[r - 1])
+                for half in range(2):
+                    sub = pl.ds(8 * half, 8)
+                    s = tiles(src[r, sub, :])
+                    below = tiles(src[r + 1, sub, :])
+                    above = tiles(src[r - 1, sub, :])
+                    w3 = tiles(winv3[r, sub, :])
+                    h = None if extra is None else tiles(extra[r, sub, :])
+                    to_east = s[1:] + [roll(s[0], -1)]
+                    flow = [e[j] * s[j] for j in range(4)]
+                    to_west = [roll(e[4] * s[4], 1)] + flow
+                    for j in range(5):
+                        t = (e[j] * to_east[j] + to_west[j]) + (south_here[j] * below[j] + south_north[j] * above[j])
+                        at = pl.ds(128 * j, 128)
+                        if image is not None:
+                            image[r, sub, at] = diag[r, sub, at] * s[j] - t
+                        if dst is not None:
+                            new = s[j] + w3[j] * t
+                            if h is not None:
+                                new = new + scale * h[j]
+                            dst[r, sub, at] = new
             return carry
 
-        lo, hi = MARGIN - width, MARGIN + CR + width
-        if image is None:
-            lax.fori_loop(0, (hi - lo) // 2, lambda i, c: plain(lo + 2 * i + 1, plain(lo + 2 * i, c)), 0)
-            return None
-        if lo < MARGIN:
-            lax.fori_loop(lo, MARGIN, plain, 0)
-            lax.fori_loop(MARGIN + CR, hi, plain, 0)
-        zero = tuple(jnp.zeros((8, 128), F32) for _ in image[1])
-
-        def rich(r, carry):
-            return cell(r, 0, carry[0]), cell(r, 1, carry[1])
-
-        top, bottom = lax.fori_loop(MARGIN, MARGIN + CR, rich, (zero, zero))
-        return [jnp.concatenate([a, b], axis=0) for a, b in zip(top, bottom)]
-
-    def block_image(field, also=None):
-        def step(r, carry):
-            acc, acc2 = carry
-            f = field[r]
-            k = kappa[r]
-            acc = acc + fold(f * jnp.concatenate([k, k], axis=0))
-            return acc, acc2
-
-        def inner(r, carry):
-            acc, acc2 = step(r, carry)
-            fi = field[r, :, 0:CC]
-            acc = acc + fold(fi * diag[r, :, 0:CC])
-            if also is not None:
-                acc2 = acc2 + fold(fi * also[r, :, 0:CC])
-            return acc, acc2
-
-        zero = jnp.zeros((NB, 128), F32)
-        carry = step(MARGIN - 1, (zero, zero))
-        carry = lax.fori_loop(MARGIN, MARGIN + CR, inner, carry, unroll=2)
-        return step(MARGIN + CR, carry)
-
-    def keep(r, carry):
-        v1[r] = s_a[r]
-        return carry
-
-    lax.fori_loop(0, WR, keep, 0, unroll=2)
-    sweep(v1, s_a, 14, extra=v1)
-    sweep(s_a, s_b, 13, extra=v1)
+        lax.fori_loop(0, count, step, 0)
+
+    def block_image(field):
+        acc = lax.fori_loop(
+            MARGIN - 1, MARGIN + CR + 1, lambda r, acc: acc + field[r] * kappa[r], wide_zero, unroll=2
+        )
+        parts = tiles(acc)
+        return (parts[0] + parts[1]) + (parts[2] + parts[3]) + parts[4]
+
+    def own_dots(*pairs):
+        def step(r, accs):
+            return tuple(acc + f[r] * g[r] for acc, (f, g) in zip(accs, pairs))
+
+        accs = lax.fori_loop(MARGIN, MARGIN + CR, step, (wide_zero,) * len(pairs), unroll=2)
+        return [fold(acc) for acc in accs]
+
+    sweep(v1, s_a, 14, v1, 3.0)
+    sweep(s_a, s_b, 13, v1, 9.0)
     send_b(0)
-    sweep(s_b, s_a, 12, extra=v1)
-    sweep(s_a, s_b, 11, extra=v1)
-    ra, ru = block_image(s_b, hsrc)
+    sweep(s_b, s_a, 12, v1, 27.0)
+    sweep(s_a, s_b, 11, v1, 81.0)
+    ra = block_image(s_b) * (1.0 / 81.0)
     zero_row = jnp.zeros((1, 128), F32)
     send_a(1, [b_row(ra, own_slot), zero_row])
+    ru = own_dots((s_b, hsrc))[0] * (1.0 / 81.0)
 
     wait_b(0)
     f0 = coarse(0, 0)
@@ -471,7 +508,7 @@
     def dot_c(a, b):
         return to_b(jnp.sum(a * b, axis=0, keepdims=True))
 
-    lane_c = iota((NB, WC), 1)
+    lane_c = jnp.broadcast_to(at_col(), (NB, WC))
 
     def around_field(y):
         fields = []
@@ -484,49 +521,58 @@
             fields.append(jnp.where(lane_c < CC, vals[0], jnp.where(lane_c < CC + 64, vals[1], vals[2])))
         return fields
 
-    def combine(dst, src, fields, width, sign):
+    def combine(dst, src, fields, width, scale):
         spans = ((MARGIN - width, MARGIN), (MARGIN, MARGIN + CR), (MARGIN + CR, MARGIN + CR + width))
         for (lo, hi), field in zip(spans, fields):
             def step(r, carry):
-                dst[r] = field + src[r] if sign > 0 else field - src[r]
+                dst[r] = field + scale * src[r]
                 return carry
-            lax.fori_loop(lo, hi, step, 0)
+            lax.fori_loop(lo, hi, step, 0, unroll=2 if (hi - lo) % 2 == 0 else 1)
 
     y0 = solve(f0)
+    combine(v0, s_b, around_field(y0), 11, 1.0 / 81.0)
+
+    sweep(v0, s_a, 10, image=w0)
     send_b(1)
-    combine(v0, s_b, around_field(y0), 11, 1)
-
-    (mu0,) = sweep(v0, s_a, 10, image=(w0, ((None, None),)))
     sweep(s_a, s_b, 9)
     sweep(s_b, s_a, 8)
     sweep(s_a, s_b, 7)
     sweep(s_b, s_a, 6)
-    ra0, _ = block_image(s_a)
+    ra0 = block_image(s_a) * (1.0 / 243.0)
     send_a(2, [b_row(ra0, own_slot), zero_row])
     wait_b(1)
     f1 = f0 + coarse(1, 0) + gap * y0
     g0 = solve(f1)
-    combine(v1, s_a, around_field(g0), 6, -1)
-
-    mu2, mu1 = sweep(v1, s_b, 5, image=(w1, ((None, None), (None, w0))))
+    combine(v1, s_a, around_field(g0), 6, -1.0 / 243.0)
+
+    sweep(v1, s_b, 5, image=w1)
     sweep(s_b, s_a, 4)
     sweep(s_a, s_b, 3)
-    send_b(2)
     sweep(s_b, s_a, 2)
     sweep(s_a, s_b, 1)
-    bab, bw1 = sweep(s_b, None, 0, image=(None, ((None, None), (None, w1))))
-    ra1, _ = block_image(s_b)
+    mu0, mu1, mu2 = own_dots((v0, w0), (v1, w0), (v1, w1))
+    sweep(s_b, None, 0, image=s_a)
+    send_b(2)
+    bab, bw1 = own_dots((s_b, s_a), (s_b, w1))
+    bab = bab * (1.0 / (243.0 * 243.0))
+    bw1 = bw1 * (1.0 / 243.0)
+    ra1 = block_image(s_b) * (1.0 / 243.0)
     moments = zero_row
     for n, acc in enumerate((ru, mu0, mu1, mu2, bw1, bab)):
         moments = moments + b_row(acc, slot == n)
     send_a(3, [b_row(ra1, own_slot), moments])
-    wait_b(2)
-    f2 = f1 - coarse(2, 0) + gap * g0
-    g1 = solve(f2)
+    for n, field in enumerate((v0, v1, s_b)):
+        if n == 1:
+            wait_b(2)
+            f2 = f1 - coarse(2, 0) + gap * g0
+            g1 = solve(f2)
+        put_natural(n, field, 0, CR // 2)
+        if n == 1:
+            send_b(3)
+        put_natural(n, field, CR // 2, CR)
     energy_y = dot_c(f0, y0)
     g1w1 = dot_c(g1, f2)
     g1gap = dot_c(g1, g1 * gap)
-    send_b(3)
     wait_b(3)
     ra1_all = coarse(3, 0)
     g1ra1 = dot_c(g1, ra1_all)
@@ -560,38 +606,36 @@
     c0 = energy / m0 - l10 * c1 - l20 * c2
     hit = jnp.logical_and(iota((8, 256), 1) // 16 == rho, sub == col)
     shift = c2 * to_b(jnp.sum(jnp.where(hit, g1, 0.0), axis=0, keepdims=True))
-    c0 = jnp.broadcast_to(c0, (NB, CC))
-    c1 = jnp.broadcast_to(c1, (NB, CC))
-    c2 = jnp.broadcast_to(c2, (NB, CC))
-    shift = jnp.broadcast_to(shift, (NB, CC))
-
-    def finish(r, carry):
-        w = r + MARGIN
-        out[r] = c0 * v0[w, :, 0:CC] + c1 * v1[w, :, 0:CC] - c2 * s_b[w, :, 0:CC] + shift
+    for n, c in enumerate((c0, c1, c2 * (-1.0 / 243.0), shift)):
+        coef[n] = jnp.broadcast_to(c, (NB, CC))
+
+    def finish(b, carry):
+        w = [coef[n, pl.ds(b, 1), :] for n in range(4)]
+        out[b] = w[0] * nat[0, b] + w[1] * nat[1, b] + (w[2] * nat[2, b] + w[3])
         return carry
 
-    lax.fori_loop(0, CR, finish, 0, unroll=2)
+    lax.fori_loop(0, NB, finish, 0)
 
 
 def shards(conductance, nodata_mask, source_index, source_current, ground_index):
     big = pltpu.VMEM((WR, NB, WC), F32)
     edge = pltpu.VMEM((WR, 8, WC), F32)
-    own = pltpu.VMEM((CR, NB, CC), F32)
     scratch = [
-        pltpu.VMEM((WR + 8, WC), F32), pltpu.VMEM((WR, 128), F32), pltpu.VMEM((WR, 128), F32),
-        big, big, big, edge, edge, edge,
-        big, big, big, big, own, own,
+        pltpu.VMEM((WR, WC), F32), pltpu.VMEM((WR, 128), F32), pltpu.VMEM((WR, 128), F32),
+        big, big, big, edge, edge, big,
+        big, big, big, big, big, big,
         pltpu.VMEM((WR, NB, 256), BF16), pltpu.VMEM((WR, NB, 768), BF16),
         pltpu.VMEM((5, 8, 8, 256), F32), pltpu.VMEM((3, 8, 8, 256), F32), pltpu.VMEM((3, 8, 8, 256), F32),
-        pltpu.VMEM((5, WR, WC), F32),
+        pltpu.VMEM((6, WR, WC), F32),
     ]
     for q in (4, 2, 2, 2):
-        scratch += [pltpu.VMEM((N_COL, q, 128), F32), pltpu.VMEM((N_ROW, N_COL, q, 128), F32)]
+        scratch += [pltpu.VMEM((N_ROW, q, 128), F32), pltpu.VMEM((N_COL, 2, q, 128), F32)]
+    scratch += [pltpu.VMEM((3, NB, CR, CC), F32), pltpu.VMEM((4, NB, CC), F32)]
     scratch += [pltpu.SemaphoreType.DMA((8,)), pltpu.SemaphoreType.DMA((8,))]
     scratch += [pltpu.SemaphoreType.DMA((4,)) for _ in range(4)]
-    voltage = pl.pallas_call(
+    return pl.pallas_call(
         body,
-        out_shape=jax.ShapeDtypeStruct((CR, NB, CC), F32),
+        out_shape=pltpu.VMEM((NB, CR, CC), F32),
         in_specs=[pl.BlockSpec(memory_space=pltpu.VMEM)] * 5,
         out_specs=pl.BlockSpec(memory_space=pltpu.VMEM),
         scratch_shapes=scratch,
@@ -599,7 +643,6 @@
             collective_id=0, has_side_effects=True, vmem_limit_bytes=56 * 1024 * 1024
         ),
     )(conductance, nodata_mask, source_index, source_current, ground_index)
-    return jnp.transpose(voltage, (1, 0, 2))
 
 
 def solution(mesh):

time: 80.1 us -> 46.4 us (0.58)
  Pallas kernels: 77 us -> 45.3 us
  local copies, waits for them, and re-layouts: 2.81 us -> 0.97 us
    pallas_call x1, Pallas kernels: 77 us -> 45.3 us  [shards(): pl.pallas_call(body, out_shape=pltpu.VMEM((NB, CR, CC), F32), in_specs=[p...]
    transpose x1 -> x0, local copies, waits for them, and re-layouts: 2.81 us -> none  [shards(): return jnp.transpose(voltage, (1, 0, 2))]
    unnamed x0 -> x1, local copies, waits for them, and re-layouts: none -> 0.97 us
where the time goes in v2:
time: 46.4 us; the launch traced here: 46.3 us
  Pallas kernels  45.3 us (98%)
  local copies, waits for them, and re-layouts  0.97 us (2%)
    pallas_call x1, Pallas kernels, shards(): pl.pallas_call(body, out_shape=pltpu.VMEM((NB, CR, CC), F32), in_specs=[p...  45.3 us
    unnamed x1, local copies, waits for them, and re-layouts  0.97 us

profile of v2, /device:TPU:1, one launch (start us, length us, event | category | flops | bytes accessed | tf_op | source)
XLA Modules:
  0.0 46.3 jit_solution(13484563205240705837)
XLA Ops:
  0.0 45.3 %shard_map.55 = f32[16,32,512]{2,1,0:T(8,128)S(1)} custom-call(f32[32,512]{1,0:T(8,128)} %cond.1, s32[32,512]{1,0:T(8,128)} %mask.1, s32[16,16]{1,0:T(8,128)} %sidx.1, f32[16,16]{1,0:T(8,128)} %scur.1, s32[16,16]{1,0:T(8,128)} %gidx.1), custom_call_target="tpu_custom_call" | custom-call | tf_op jit(solution)/shard_map/pallas_call | solution.py:636
  45.3 1.0 %copy.7 = f32[16,32,512]{2,1,0:T(8,128)} copy(f32[16,32,512]{2,1,0:T(8,128)S(1)} %shard_map.55) | data formatting | bytes 2097152

commit v3 on v2

--- a/solution.py
+++ b/solution.py
@@ -14,7 +14,8 @@
 N_COL = 8
 NC = N_COL * CC
 MARGIN = 16
-STEP_ROWS = 6
+EARLY = 24
+CHOICES = (6, 12)
 WR = CR + 2 * MARGIN
 WC = CC + 128
 F32 = jnp.float32
@@ -121,7 +122,8 @@
 
 
 def body(
-    cond, mask, sidx, scur, gidx, out,
+    cond_hbm, mask_hbm, sidx_hbm, scur_hbm, gidx_hbm, out,
+    cond, mask, sidx, scur, gidx, in_sem,
     mwin, side_r, side_l, diag, hsrc, winv3, e_east, e_south, kappa,
     s_a, s_b, v0, v1, w0, w1, lhs_g, lhs_s, cfac, clow, cup, mrow,
     ga0, gb0, ga1, gb1, ga2, gb2, ga3, gb3,
@@ -152,6 +154,16 @@
         def _():
             pl.semaphore_signal(barrier, inc=1, device_id=(rho + dr, col + dc), device_id_type=MESH)
 
+    fetches = [
+        pltpu.make_async_copy(far, near, in_sem.at[n])
+        for n, (far, near) in enumerate((
+            (cond_hbm, cond), (mask_hbm, mask), (gidx_hbm, gidx), (sidx_hbm, sidx), (scur_hbm, scur),
+        ))
+    ]
+    for fetch in fetches:
+        fetch.start()
+    for fetch in fetches:
+        fetch.wait()
     mwin[MARGIN : MARGIN + CR, 0:CC] = cond[...] * mask[...].astype(F32)
 
     def land(dr, dc):
@@ -180,21 +192,21 @@
             device_id=(rho + dr, col + dc), device_id_type=MESH,
         )
 
+    expected = N_COL - 1 + N_ROW - 1
+    for dr, dc in diagonals:
+        expected = expected + exists(dr, dc).astype(jnp.int32)
+    pl.semaphore_wait(barrier, expected)
+
+    for n, (dr, dc) in enumerate(around):
+        @pl.when(exists(dr, dc))
+        def _():
+            halo_copy(n, dr, dc).start()
+
     gflat = flat_row(gidx[...].astype(F32)).astype(jnp.int32)
     sflat = flat_row(sidx[...].astype(F32)).astype(jnp.int32)
     cflat = flat_row(scur[...])
     g_row, g_col = gflat // NC, gflat % NC
     s_row, s_col = sflat // NC, sflat % NC
-
-    expected = N_COL - 1 + N_ROW - 1
-    for dr, dc in diagonals:
-        expected = expected + exists(dr, dc).astype(jnp.int32)
-    pl.semaphore_wait(barrier, expected)
-
-    for n, (dr, dc) in enumerate(around):
-        @pl.when(exists(dr, dc))
-        def _():
-            halo_copy(n, dr, dc).start()
 
     own_b = iota((NB, 256), 1) // 16 == iota((NB, 256), 0)
     g_rel = g_row - rho * CR + MARGIN
@@ -244,6 +256,38 @@
             iota((256, 256), 1) // 16 == iota((256, 256), 0) % 16,
         ), 1.0, 0.0).astype(BF16)
     shunt_total = lax.dot_general(a1, a2, NT, preferred_element_type=F32)
+
+    mrow[3, MARGIN : MARGIN + CR, :] = jnp.where(
+        interleave(jnp.concatenate([mwin[MARGIN : MARGIN + CR, 0:CC], jnp.zeros((CR, 128), F32)], axis=1)) > 0.0,
+        1.0, 0.0,
+    )
+    wide_zero = jnp.zeros((NB, WC), F32)
+    inflow_acc = lax.fori_loop(
+        MARGIN, MARGIN + CR, lambda r, acc: acc + hsrc[r] * mrow[3, pl.ds(r, 1), :], wide_zero, unroll=4
+    )
+
+    def total(field):
+        return jnp.sum(jnp.sum(field, axis=0, keepdims=True), axis=1, keepdims=True)
+
+    slot = iota((NB, 128), 1) // 16
+    own_slot = slot == lax.rem(rho, 8)
+    same_b = iota((NB, 128), 1) % 16 == iota((NB, 128), 0)
+    row_slot = iota((1, 128), 1) // 16 == lax.rem(rho, 8)
+
+    def one_row(value):
+        return jnp.where(row_slot, jnp.broadcast_to(value, (1, 128)), 0.0)
+
+    def b_row(acc, where):
+        value = jnp.sum(acc, axis=1, keepdims=True)
+        return jnp.sum(jnp.where(jnp.logical_and(where, same_b), value, 0.0), axis=0, keepdims=True)
+
+    own_col = at_col() < CC
+
+    def fold(x):
+        parts = tiles(jnp.where(own_col, x, 0.0))
+        return parts[0] + parts[1] + ((parts[2] + parts[3]) + parts[4])
+
+    inflow_row = b_row(fold(inflow_acc), own_slot)
 
     for n, (dr, dc) in enumerate(around):
         @pl.when(exists(dr, dc))
@@ -281,41 +325,18 @@
     col_in_e = jnp.where(jnp.logical_or(at_c < CC - 1, at_c == WC - 1), 1.0, 0.0)
     col_in_w = jnp.where(jnp.logical_and(at_c >= 1, at_c <= CC), 1.0, 0.0)
     inside = row_in * col_in
-    mrow[4] = (
-        base * inside - east * (row_in * col_in_e) - west * (row_in * col_in_w)
-        - south * (row_in_s * col_in) - north * (row_in_n * col_in)
-    )
-    mrow[5] = inside
     gap_field = ((((base - east) - west) - south) - north - LEAKAGE) * inside
     east_field = jnp.where(at_c == CC - 1, east * row_in, 0.0)
     south_field = jnp.where(at_r == MARGIN + CR - 1, south * col_in, 0.0)
 
-    def total(field):
-        return jnp.sum(jnp.sum(field, axis=0, keepdims=True), axis=1, keepdims=True)
-
-    slot = iota((NB, 128), 1) // 16
-    own_slot = slot == lax.rem(rho, 8)
-    same_b = iota((NB, 128), 1) % 16 == iota((NB, 128), 0)
-    row_slot = iota((1, 128), 1) // 16 == lax.rem(rho, 8)
-
-    def one_row(value):
-        return jnp.where(row_slot, jnp.broadcast_to(value, (1, 128)), 0.0)
-
-    def b_row(acc, where):
-        value = jnp.sum(acc, axis=1, keepdims=True)
-        return jnp.sum(jnp.where(jnp.logical_and(where, same_b), value, 0.0), axis=0, keepdims=True)
-
-    own_col = at_col() < CC
-
-    def fold(x):
-        parts = tiles(jnp.where(own_col, x, 0.0))
-        return parts[0] + parts[1] + ((parts[2] + parts[3]) + parts[4])
-
-    def put_natural(n, field, lo, hi):
+    def put_natural(n, field, lo, hi, less=None):
         def step(r, carry):
             for half in range(2):
                 sub = pl.ds(8 * half, 8)
-                nat[n, sub, r, :] = natural(tiles(field[r + MARGIN, sub, :]))
+                value = field[r + MARGIN, sub, :]
+                if less is not None:
+                    value = 81.0 * (value - less[8 * half : 8 * half + 8])
+                nat[n, sub, r, :] = natural(tiles(value))
             return carry
 
         lax.fori_loop(lo, hi, step, 0, unroll=4)
@@ -359,16 +380,15 @@
         gb = gbs[g]
         return jnp.concatenate([gb[:, 0, k, :], gb[:, 1, k, :]], axis=1)
 
-    def mask_rows(r, carry):
-        here = hsrc[r] * mrow[3, pl.ds(r, 1), :]
-        hsrc[r] = here
-        return carry + here * mrow[5, pl.ds(r, 1), :]
-
-    wide_zero = jnp.zeros((NB, WC), F32)
-    inflow_acc = lax.fori_loop(0, WR, mask_rows, wide_zero, unroll=4)
     send_a(0, [
-        b_row(fold(inflow_acc), own_slot), one_row(total(east_field)), one_row(total(south_field)), one_row(total(gap_field)),
+        inflow_row, one_row(total(east_field)), one_row(total(south_field)), one_row(total(gap_field)),
     ])
+
+    mrow[4] = (
+        base * inside - east * (row_in * col_in_e) - west * (row_in * col_in_w)
+        - south * (row_in_s * col_in) - north * (row_in_n * col_in)
+    )
+    mrow[5] = inside
 
     def coeffs(r, carry):
         rows = pl.ds(r, 1)
@@ -378,7 +398,9 @@
         diag[r] = d
         winv3[r] = inverse
         kappa[r] = mrow[4, rows, :] + shunt * mrow[5, rows, :]
-        v1[r] = (1.0 / 3.0) * inverse * hsrc[r]
+        here = hsrc[r] * mrow[3, rows, :]
+        hsrc[r] = here
+        v1[r] = (1.0 / 3.0) * inverse * here
         e_east[r] = jnp.broadcast_to(mrow[2, rows, :], (8, WC))
         e_south[r] = jnp.broadcast_to(mrow[0, rows, :], (8, WC))
         return carry
@@ -386,12 +408,14 @@
     lax.fori_loop(0, WR, coeffs, 0, unroll=2)
 
     def sweep(src, dst, width, extra=None, scale=None, image=None):
-        count = -(-(CR + 2 * width) // STEP_ROWS)
-        lo = MARGIN - width - (count * STEP_ROWS - CR - 2 * width) // 2
+        rows = CR + 2 * width
+        at_once = min(range(CHOICES[0], CHOICES[1]), key=lambda n: (-(-rows // n) * n, -n))
+        count = -(-rows // at_once)
+        lo = MARGIN - width - (count * at_once - rows) // 2
 
         def step(i, carry):
-            r0 = lo + i * STEP_ROWS
-            for k in range(STEP_ROWS):
+            r0 = lo + i * at_once
+            for k in range(at_once):
                 r = r0 + k
                 e = tiles(e_east[r])
                 south_here = tiles(e_south[r])
@@ -436,14 +460,15 @@
 
     sweep(v1, s_a, 14, v1, 3.0)
     sweep(s_a, s_b, 13, v1, 9.0)
+    sweep(s_b, s_a, 12, v1, 27.0)
     send_b(0)
-    sweep(s_b, s_a, 12, v1, 27.0)
     sweep(s_a, s_b, 11, v1, 81.0)
     ra = block_image(s_b) * (1.0 / 81.0)
     zero_row = jnp.zeros((1, 128), F32)
     send_a(1, [b_row(ra, own_slot), zero_row])
     ru = own_dots((s_b, hsrc))[0] * (1.0 / 81.0)
 
+    put_natural(0, s_b, 0, EARLY)
     wait_b(0)
     f0 = coarse(0, 0)
     ec = coarse(0, 1)
@@ -527,7 +552,7 @@
             def step(r, carry):
                 dst[r] = field + scale * src[r]
                 return carry
-            lax.fori_loop(lo, hi, step, 0, unroll=2 if (hi - lo) % 2 == 0 else 1)
+            lax.fori_loop(lo, hi, step, 0, unroll=hi - lo if hi - lo < 16 else 4)
 
     y0 = solve(f0)
     combine(v0, s_b, around_field(y0), 11, 1.0 / 81.0)
@@ -561,15 +586,21 @@
     for n, acc in enumerate((ru, mu0, mu1, mu2, bw1, bab)):
         moments = moments + b_row(acc, slot == n)
     send_a(3, [b_row(ra1, own_slot), moments])
-    for n, field in enumerate((v0, v1, s_b)):
-        if n == 1:
-            wait_b(2)
-            f2 = f1 - coarse(2, 0) + gap * g0
-            g1 = solve(f2)
-        put_natural(n, field, 0, CR // 2)
-        if n == 1:
-            send_b(3)
-        put_natural(n, field, CR // 2, CR)
+    own_block = jnp.logical_and(iota((8, 256), 1) // 16 == rho, sub == col)
+
+    def own_value(y):
+        return to_b(jnp.sum(jnp.where(own_block, y, 0.0), axis=0, keepdims=True))
+
+    y0_own = own_value(y0)
+    put_natural(1, v1, 0, CR)
+    wait_b(2)
+    f2 = f1 - coarse(2, 0) + gap * g0
+    g1 = solve(f2)
+    put_natural(2, s_b, 0, CR // 2)
+    send_b(3)
+    put_natural(2, s_b, CR // 2, CR)
+    put_natural(0, v0, EARLY, CR, jnp.broadcast_to(y0_own, (NB, WC)))
+    g1_own = own_value(g1)
     energy_y = dot_c(f0, y0)
     g1w1 = dot_c(g1, f2)
     g1gap = dot_c(g1, g1 * gap)
@@ -604,9 +635,8 @@
     c2 = ratio(t2, d2, 0.0)
     c1 = ratio(t1, d1, 0.0) - l21 * c2
     c0 = energy / m0 - l10 * c1 - l20 * c2
-    hit = jnp.logical_and(iota((8, 256), 1) // 16 == rho, sub == col)
-    shift = c2 * to_b(jnp.sum(jnp.where(hit, g1, 0.0), axis=0, keepdims=True))
-    for n, c in enumerate((c0, c1, c2 * (-1.0 / 243.0), shift)):
+    shift = c0 * y0_own + c2 * g1_own
+    for n, c in enumerate((c0 * (1.0 / 81.0), c1, c2 * (-1.0 / 243.0), shift)):
         coef[n] = jnp.broadcast_to(c, (NB, CC))
 
     def finish(b, carry):
@@ -621,6 +651,8 @@
     big = pltpu.VMEM((WR, NB, WC), F32)
     edge = pltpu.VMEM((WR, 8, WC), F32)
     scratch = [
+        pltpu.VMEM((CR, CC), F32), pltpu.VMEM((CR, CC), jnp.int32), pltpu.VMEM((NB, 16), jnp.int32),
+        pltpu.VMEM((NB, 16), F32), pltpu.VMEM((NB, 16), jnp.int32), pltpu.SemaphoreType.DMA((5,)),
         pltpu.VMEM((WR, WC), F32), pltpu.VMEM((WR, 128), F32), pltpu.VMEM((WR, 128), F32),
         big, big, big, edge, edge, big,
         big, big, big, big, big, big,
@@ -636,7 +668,7 @@
     return pl.pallas_call(
         body,
         out_shape=pltpu.VMEM((NB, CR, CC), F32),
-        in_specs=[pl.BlockSpec(memory_space=pltpu.VMEM)] * 5,
+        in_specs=[pl.BlockSpec(memory_space=pltpu.HBM)] * 5,
         out_specs=pl.BlockSpec(memory_space=pltpu.VMEM),
         scratch_shapes=scratch,
         compiler_params=pltpu.CompilerParams(

time: 46.4 us -> 43.7 us (0.942)
  Pallas kernels: 45.3 us -> 42.6 us
    pallas_call x1, Pallas kernels: 45.3 us -> 42.6 us  [shards(): pl.pallas_call(body, out_shape=pltpu.VMEM((NB, CR, CC), F32), in_specs=[p...]
where the time goes in v3:
time: 43.7 us; the launch traced here: 43.6 us
  Pallas kernels  42.6 us (97%)
  local copies, waits for them, and re-layouts  0.97 us (2%)
    pallas_call x1, Pallas kernels, shards(): pl.pallas_call(body, out_shape=pltpu.VMEM((NB, CR, CC), F32), in_specs=[p...  42.6 us
    unnamed x1, local copies, waits for them, and re-layouts  0.97 us

profile of v3, /device:TPU:1, one launch (start us, length us, event | category | flops | bytes accessed | tf_op | source)
XLA Modules:
  0.0 43.6 jit_solution(13445457507595264858)
XLA Ops:
  0.0 42.6 %shard_map.55 = f32[16,32,512]{2,1,0:T(8,128)S(1)} custom-call(f32[32,512]{1,0:T(8,128)} %cond_hbm.1, s32[32,512]{1,0:T(8,128)} %mask_hbm.1, s32[16,16]{1,0:T(8,128)} %sidx_hbm.1, f32[16,16]{1,0:T(8,128)} %scur_hbm.1, s32[16,16]{1,0:T(8,128)} %gidx_hbm.1), custom_call_target="tpu_custom_call" | custom-call | tf_op jit(solution)/shard_map/pallas_call | solution.py:668
  42.6 1.0 %copy.7 = f32[16,32,512]{2,1,0:T(8,128)} copy(f32[16,32,512]{2,1,0:T(8,128)S(1)} %shard_map.55) | data formatting | bytes 2097152

commit v4 on v3

--- a/solution.py
+++ b/solution.py
@@ -14,7 +14,7 @@
 N_COL = 8
 NC = N_COL * CC
 MARGIN = 16
-EARLY = 24
+EARLY = 16
 CHOICES = (6, 12)
 WR = CR + 2 * MARGIN
 WC = CC + 128
@@ -166,41 +166,58 @@
         fetch.wait()
     mwin[MARGIN : MARGIN + CR, 0:CC] = cond[...] * mask[...].astype(F32)
 
-    def land(dr, dc):
+    near = ((-1, 0, 0), (1, 0, 0), (0, -1, 0), (0, 1, 0))
+    far = ((-1, 0, 1), (1, 0, 1)) + tuple((dr, dc, 1) for dr, dc in diagonals)
+    around = near + far
+
+    def land(dr, dc, part):
+        if dc == 0:
+            first = (8 - 8 * part) if dr < 0 else MARGIN + CR + 8 * part
+            return mwin.at[pl.ds(first, 8), pl.ds(0, CC)]
         rows = {-1: pl.ds(0, MARGIN), 0: pl.ds(MARGIN, CR), 1: pl.ds(MARGIN + CR, MARGIN)}[dr]
+        return (side_r if dc > 0 else side_l).at[rows, :]
+
+    def take(dr, dc, part):
         if dc == 0:
-            return mwin.at[rows, pl.ds(0, CC)]
-        return (side_r if dc > 0 else side_l).at[rows, :]
-
-    def take(dr, dc):
-        rows = {-1: pl.ds(MARGIN, MARGIN), 0: pl.ds(MARGIN, CR), 1: pl.ds(MARGIN + CR - MARGIN, MARGIN)}[dr]
-        cols = {-1: pl.ds(0, 128), 0: pl.ds(0, CC), 1: pl.ds(CC - 128, 128)}[dc]
-        return mwin.at[rows, cols]
-
-    around = [(dr, dc) for dr in (-1, 0, 1) for dc in (-1, 0, 1) if dr or dc]
-    for dr, dc in around:
+            first = (MARGIN + 8 * part) if dr < 0 else MARGIN + CR - 8 - 8 * part
+            return mwin.at[pl.ds(first, 8), pl.ds(0, CC)]
+        rows = {-1: pl.ds(MARGIN, MARGIN), 0: pl.ds(MARGIN, CR), 1: pl.ds(CR, MARGIN)}[dr]
+        return mwin.at[rows, pl.ds(0, 128) if dc < 0 else pl.ds(CC - 128, 128)]
+
+    for dr, dc, part in around:
         @pl.when(jnp.logical_not(exists(dr, dc)))
         def _():
-            ref = land(dr, dc)
+            ref = land(dr, dc, part)
             ref[...] = jnp.zeros(ref.shape, F32)
 
-    def halo_copy(n, dr, dc):
-        m = around.index((-dr, -dc))
-        return pltpu.make_async_remote_copy(
-            src_ref=take(dr, dc), dst_ref=land(-dr, -dc),
-            send_sem=halo_send.at[n], recv_sem=halo_recv.at[m],
-            device_id=(rho + dr, col + dc), device_id_type=MESH,
-        )
+    def halo_start(n):
+        dr, dc, part = around[n]
+        m = around.index((-dr, -dc, part))
+        @pl.when(exists(dr, dc))
+        def _():
+            pltpu.make_async_remote_copy(
+                src_ref=take(dr, dc, part), dst_ref=land(-dr, -dc, part),
+                send_sem=halo_send.at[n], recv_sem=halo_recv.at[m],
+                device_id=(rho + dr, col + dc), device_id_type=MESH,
+            ).start()
+
+    def halo_wait(n):
+        dr, dc, part = around[n]
+        @pl.when(exists(dr, dc))
+        def _():
+            pltpu.make_async_remote_copy(
+                src_ref=take(dr, dc, part), dst_ref=land(dr, dc, part),
+                send_sem=halo_send.at[n], recv_sem=halo_recv.at[n],
+                device_id=(rho + dr, col + dc), device_id_type=MESH,
+            ).wait()
 
     expected = N_COL - 1 + N_ROW - 1
     for dr, dc in diagonals:
         expected = expected + exists(dr, dc).astype(jnp.int32)
     pl.semaphore_wait(barrier, expected)
 
-    for n, (dr, dc) in enumerate(around):
-        @pl.when(exists(dr, dc))
-        def _():
-            halo_copy(n, dr, dc).start()
+    for n in range(len(around)):
+        halo_start(n)
 
     gflat = flat_row(gidx[...].astype(F32)).astype(jnp.int32)
     sflat = flat_row(sidx[...].astype(F32)).astype(jnp.int32)
@@ -224,7 +241,7 @@
         lhs_s[r, :, 512:768] = jnp.where(s_hit, c_lo, 0.0).astype(BF16)
         return carry
 
-    lax.fori_loop(0, WR, build, 0)
+    lax.fori_loop(0, WR, build, 0, unroll=4)
 
     def place(column):
         rel = column - col * CC
@@ -235,7 +252,7 @@
     s_one = jnp.where(place(s_col) == spot, 1.0, 0.0).astype(BF16)
     s_hot = jnp.concatenate([s_one, s_one, s_one], axis=1)
 
-    STEP = 16
+    STEP = 32
 
     def spread(i, carry):
         rows = pl.ds(i * STEP, STEP)
@@ -289,16 +306,83 @@
 
     inflow_row = b_row(fold(inflow_acc), own_slot)
 
-    for n, (dr, dc) in enumerate(around):
-        @pl.when(exists(dr, dc))
-        def _():
-            halo_copy(n, dr, dc).wait_send()
-            ref = land(dr, dc)
+    def put_natural(n, field, lo, hi, less=None):
+        def step(r, carry):
+            for half in range(2):
+                sub = pl.ds(8 * half, 8)
+                value = field[r + MARGIN, sub, :]
+                if less is not None:
+                    value = 81.0 * (value - less[8 * half : 8 * half + 8])
+                nat[n, sub, r, :] = natural(tiles(value))
+            return carry
+
+        lax.fori_loop(lo, hi, step, 0, unroll=4)
+
+    def send_a(g, rows):
+        ga = gas[g]
+        ga[rho] = jnp.concatenate(rows, axis=0)
+        for i in range(1, N_ROW):
             pltpu.make_async_remote_copy(
-                src_ref=ref, dst_ref=ref, send_sem=halo_send.at[n], recv_sem=halo_recv.at[n],
-                device_id=(rho + dr, col + dc), device_id_type=MESH,
-            ).wait_recv()
+                src_ref=ga.at[rho], dst_ref=ga.at[rho], send_sem=ga_send.at[g], recv_sem=ga_recv.at[g],
+                device_id=(lax.rem(rho + i, N_ROW), col), device_id_type=MESH,
+            ).start()
+
+    def send_b(g):
+        ga, gb = gas[g], gbs[g]
+        peers = pl.ds(0, N_ROW - 1)
+        pltpu.make_async_remote_copy(
+            src_ref=ga.at[peers], dst_ref=ga.at[peers], send_sem=ga_send.at[g], recv_sem=ga_recv.at[g],
+            device_id=(lax.rem(rho + 1, N_ROW), col), device_id_type=MESH,
+        ).wait()
+        for h in range(2):
+            acc = ga[8 * h]
+            for i in range(1, 8):
+                acc = acc + ga[8 * h + i]
+            gb[col, h] = acc
+        for i in range(1, N_COL):
+            pltpu.make_async_remote_copy(
+                src_ref=gb.at[col], dst_ref=gb.at[col], send_sem=gb_send.at[g], recv_sem=gb_recv.at[g],
+                device_id=(rho, lax.rem(col + i, N_COL)), device_id_type=MESH,
+            ).start()
+
+    def wait_b(g):
+        gb = gbs[g]
+        peers = pl.ds(0, N_COL - 1)
+        pltpu.make_async_remote_copy(
+            src_ref=gb.at[peers], dst_ref=gb.at[peers], send_sem=gb_send.at[g], recv_sem=gb_recv.at[g],
+            device_id=(rho, lax.rem(col + 1, N_COL)), device_id_type=MESH,
+        ).wait()
+
+    def coarse(g, k):
+        gb = gbs[g]
+        return jnp.concatenate([gb[:, 0, k, :], gb[:, 1, k, :]], axis=1)
+
+    for n in range(len(near)):
+        halo_wait(n)
+    inner = slice(MARGIN, MARGIN + CR)
     lane = iota((WR, 128), 1)
+    beside = jnp.where(lane[0:CR] < 64, side_r[inner, :], side_l[inner, :])
+    m = jnp.concatenate([mwin[inner, 0:CC], beside], axis=1)
+
+    def held_of(x):
+        return jnp.where(x > 0.0, 1.0, 0.0)
+
+    present = held_of(m)
+    east = 0.5 * present * roll(present, -1) * (m + roll(m, -1))
+    west = roll(east, 1)[:, 0:CC]
+    east = east[:, 0:CC]
+    m, present = m[:, 0:CC], present[:, 0:CC]
+    m_s, m_n = mwin[MARGIN + 1 : MARGIN + CR + 1, 0:CC], mwin[MARGIN - 1 : MARGIN + CR - 1, 0:CC]
+    south = 0.5 * present * held_of(m_s) * (m + m_s)
+    north = 0.5 * held_of(m_n) * present * (m_n + m)
+    base = east + west + south + north + LEAKAGE
+    gap_total = total((((base - east) - west) - south) - north - LEAKAGE)
+    east_total = jnp.sum(east[:, CC - 1 : CC], axis=0, keepdims=True)
+    south_total = jnp.sum(south[CR - 1 : CR, :], axis=1, keepdims=True)
+    send_a(0, [inflow_row, one_row(east_total), one_row(south_total), one_row(gap_total)])
+
+    for n in range(len(near), len(around)):
+        halo_wait(n)
     mwin[0:WR, CC:WC] = jnp.where(lane < 64, side_r[...], side_l[...])
 
     m = interleave(mwin[...])
@@ -325,64 +409,6 @@
     col_in_e = jnp.where(jnp.logical_or(at_c < CC - 1, at_c == WC - 1), 1.0, 0.0)
     col_in_w = jnp.where(jnp.logical_and(at_c >= 1, at_c <= CC), 1.0, 0.0)
     inside = row_in * col_in
-    gap_field = ((((base - east) - west) - south) - north - LEAKAGE) * inside
-    east_field = jnp.where(at_c == CC - 1, east * row_in, 0.0)
-    south_field = jnp.where(at_r == MARGIN + CR - 1, south * col_in, 0.0)
-
-    def put_natural(n, field, lo, hi, less=None):
-        def step(r, carry):
-            for half in range(2):
-                sub = pl.ds(8 * half, 8)
-                value = field[r + MARGIN, sub, :]
-                if less is not None:
-                    value = 81.0 * (value - less[8 * half : 8 * half + 8])
-                nat[n, sub, r, :] = natural(tiles(value))
-            return carry
-
-        lax.fori_loop(lo, hi, step, 0, unroll=4)
-
-    def send_a(g, rows):
-        ga = gas[g]
-        ga[rho] = jnp.concatenate(rows, axis=0)
-        for i in range(1, N_ROW):
-            pltpu.make_async_remote_copy(
-                src_ref=ga.at[rho], dst_ref=ga.at[rho], send_sem=ga_send.at[g], recv_sem=ga_recv.at[g],
-                device_id=(lax.rem(rho + i, N_ROW), col), device_id_type=MESH,
-            ).start()
-
-    def send_b(g):
-        ga, gb = gas[g], gbs[g]
-        peers = pl.ds(0, N_ROW - 1)
-        pltpu.make_async_remote_copy(
-            src_ref=ga.at[peers], dst_ref=ga.at[peers], send_sem=ga_send.at[g], recv_sem=ga_recv.at[g],
-            device_id=(lax.rem(rho + 1, N_ROW), col), device_id_type=MESH,
-        ).wait()
-        for h in range(2):
-            acc = ga[8 * h]
-            for i in range(1, 8):
-                acc = acc + ga[8 * h + i]
-            gb[col, h] = acc
-        for i in range(1, N_COL):
-            pltpu.make_async_remote_copy(
-                src_ref=gb.at[col], dst_ref=gb.at[col], send_sem=gb_send.at[g], recv_sem=gb_recv.at[g],
-                device_id=(rho, lax.rem(col + i, N_COL)), device_id_type=MESH,
-            ).start()
-
-    def wait_b(g):
-        gb = gbs[g]
-        peers = pl.ds(0, N_COL - 1)
-        pltpu.make_async_remote_copy(
-            src_ref=gb.at[peers], dst_ref=gb.at[peers], send_sem=gb_send.at[g], recv_sem=gb_recv.at[g],
-            device_id=(rho, lax.rem(col + 1, N_COL)), device_id_type=MESH,
-        ).wait()
-
-    def coarse(g, k):
-        gb = gbs[g]
-        return jnp.concatenate([gb[:, 0, k, :], gb[:, 1, k, :]], axis=1)
-
-    send_a(0, [
-        inflow_row, one_row(total(east_field)), one_row(total(south_field)), one_row(total(gap_field)),
-    ])
 
     mrow[4] = (
         base * inside - east * (row_in * col_in_e) - west * (row_in * col_in_w)
@@ -390,22 +416,36 @@
     )
     mrow[5] = inside
 
-    def coeffs(r, carry):
+    def coeffs(r, inner):
         rows = pl.ds(r, 1)
         shunt = diag[r]
         d = shunt + mrow[1, rows, :]
         inverse = 2.0 / d
-        diag[r] = d
+        here = hsrc[r] * mrow[3, rows, :]
         winv3[r] = inverse
-        kappa[r] = mrow[4, rows, :] + shunt * mrow[5, rows, :]
-        here = hsrc[r] * mrow[3, rows, :]
-        hsrc[r] = here
         v1[r] = (1.0 / 3.0) * inverse * here
         e_east[r] = jnp.broadcast_to(mrow[2, rows, :], (8, WC))
         e_south[r] = jnp.broadcast_to(mrow[0, rows, :], (8, WC))
+        if inner:
+            diag[r] = d
+            hsrc[r] = here
+            kappa[r] = mrow[4, rows, :] + shunt * mrow[5, rows, :]
+
+    def coeffs_rim(i, carry):
+        coeffs(1 + i, False)
+        coeffs(MARGIN + CR + i, False)
         return carry
 
-    lax.fori_loop(0, WR, coeffs, 0, unroll=2)
+    def coeffs_block(i, carry):
+        coeffs(MARGIN + 2 * i, True)
+        coeffs(MARGIN + 2 * i + 1, True)
+        return carry
+
+    e_south[0] = jnp.broadcast_to(mrow[0, 0:1, :], (8, WC))
+    lax.fori_loop(0, MARGIN - 1, coeffs_rim, 0)
+    lax.fori_loop(0, CR // 2, coeffs_block, 0)
+    for r in (MARGIN - 1, MARGIN + CR):
+        kappa[r] = jnp.broadcast_to(mrow[4, r : r + 1, :], (NB, WC))
 
     def sweep(src, dst, width, extra=None, scale=None, image=None):
         rows = CR + 2 * width
@@ -565,6 +605,7 @@
     sweep(s_b, s_a, 6)
     ra0 = block_image(s_a) * (1.0 / 243.0)
     send_a(2, [b_row(ra0, own_slot), zero_row])
+    (mu0,) = own_dots((v0, w0))
     wait_b(1)
     f1 = f0 + coarse(1, 0) + gap * y0
     g0 = solve(f1)
@@ -575,7 +616,7 @@
     sweep(s_a, s_b, 3)
     sweep(s_b, s_a, 2)
     sweep(s_a, s_b, 1)
-    mu0, mu1, mu2 = own_dots((v0, w0), (v1, w0), (v1, w1))
+    mu1, mu2 = own_dots((v1, w0), (v1, w1))
     sweep(s_b, None, 0, image=s_a)
     send_b(2)
     bab, bw1 = own_dots((s_b, s_a), (s_b, w1))
@@ -663,7 +704,7 @@
     for q in (4, 2, 2, 2):
         scratch += [pltpu.VMEM((N_ROW, q, 128), F32), pltpu.VMEM((N_COL, 2, q, 128), F32)]
     scratch += [pltpu.VMEM((3, NB, CR, CC), F32), pltpu.VMEM((4, NB, CC), F32)]
-    scratch += [pltpu.SemaphoreType.DMA((8,)), pltpu.SemaphoreType.DMA((8,))]
+    scratch += [pltpu.SemaphoreType.DMA((10,)), pltpu.SemaphoreType.DMA((10,))]
     scratch += [pltpu.SemaphoreType.DMA((4,)) for _ in range(4)]
     return pl.pallas_call(
         body,

time: 43.7 us -> 43.1 us (0.986)
  Pallas kernels: 42.6 us -> 41.9 us
    pallas_call x1, Pallas kernels: 42.6 us -> 41.9 us  [shards(): pl.pallas_call(body, out_shape=pltpu.VMEM((NB, CR, CC), F32), in_specs=[p...]
where the time goes in v4:
time: 43.1 us; the launch traced here: 42.9 us
  Pallas kernels  41.9 us (97%)
  local copies, waits for them, and re-layouts  0.97 us (2%)
    pallas_call x1, Pallas kernels, shards(): pl.pallas_call(body, out_shape=pltpu.VMEM((NB, CR, CC), F32), in_specs=[p...  41.9 us
    unnamed x1, local copies, waits for them, and re-layouts  0.97 us

profile of v4, /device:TPU:1, one launch (start us, length us, event | category | flops | bytes accessed | tf_op | source)
XLA Modules:
  0.0 42.9 jit_solution(1652891669837454494)
XLA Ops:
  0.0 41.9 %shard_map.55 = f32[16,32,512]{2,1,0:T(8,128)S(1)} custom-call(f32[32,512]{1,0:T(8,128)} %cond_hbm.1, s32[32,512]{1,0:T(8,128)} %mask_hbm.1, s32[16,16]{1,0:T(8,128)} %sidx_hbm.1, f32[16,16]{1,0:T(8,128)} %scur_hbm.1, s32[16,16]{1,0:T(8,128)} %gidx_hbm.1), custom_call_target="tpu_custom_call" | custom-call | tf_op jit(solution)/shard_map/pallas_call | solution.py:709
  42.0 1.0 %copy.7 = f32[16,32,512]{2,1,0:T(8,128)} copy(f32[16,32,512]{2,1,0:T(8,128)S(1)} %shard_map.55) | data formatting | bytes 2097152

commit v5 on v4

--- a/solution.py
+++ b/solution.py
@@ -318,13 +318,23 @@
 
         lax.fori_loop(lo, hi, step, 0, unroll=4)
 
+    def ring(d):
+        return min(d, 4 - d)
+
+    slow, fast = rho // 4, lax.rem(rho, 4)
+    row_steps = sorted(((a, b) for a in range(4) for b in range(4) if a or b), key=lambda t: -ring(t[0]) - ring(t[1]))
+    row_peers = [lax.rem(slow + a, 4) * 4 + lax.rem(fast + b, 4) for a, b in row_steps]
+    chip, core = col // 2, lax.rem(col, 2)
+    col_steps = sorted(((a, b) for a in range(4) for b in range(2) if a or b), key=lambda t: (-ring(t[0]), -t[1]))
+    col_peers = [lax.rem(chip + a, 4) * 2 + lax.rem(core + b, 2) for a, b in col_steps]
+
     def send_a(g, rows):
         ga = gas[g]
         ga[rho] = jnp.concatenate(rows, axis=0)
-        for i in range(1, N_ROW):
+        for peer in row_peers:
             pltpu.make_async_remote_copy(
                 src_ref=ga.at[rho], dst_ref=ga.at[rho], send_sem=ga_send.at[g], recv_sem=ga_recv.at[g],
-                device_id=(lax.rem(rho + i, N_ROW), col), device_id_type=MESH,
+                device_id=(peer, col), device_id_type=MESH,
             ).start()
 
     def send_b(g):
@@ -339,10 +349,10 @@
             for i in range(1, 8):
                 acc = acc + ga[8 * h + i]
             gb[col, h] = acc
-        for i in range(1, N_COL):
+        for peer in col_peers:
             pltpu.make_async_remote_copy(
                 src_ref=gb.at[col], dst_ref=gb.at[col], send_sem=gb_send.at[g], recv_sem=gb_recv.at[g],
-                device_id=(rho, lax.rem(col + i, N_COL)), device_id_type=MESH,
+                device_id=(rho, peer), device_id_type=MESH,
             ).start()
 
     def wait_b(g):
@@ -495,7 +505,7 @@
         def step(r, accs):
             return tuple(acc + f[r] * g[r] for acc, (f, g) in zip(accs, pairs))
 
-        accs = lax.fori_loop(MARGIN, MARGIN + CR, step, (wide_zero,) * len(pairs), unroll=2)
+        accs = lax.fori_loop(MARGIN, MARGIN + CR, step, (wide_zero,) * len(pairs), unroll=4)
         return [fold(acc) for acc in accs]
 
     sweep(v1, s_a, 14, v1, 3.0)
@@ -685,7 +695,7 @@
         out[b] = w[0] * nat[0, b] + w[1] * nat[1, b] + (w[2] * nat[2, b] + w[3])
         return carry
 
-    lax.fori_loop(0, NB, finish, 0)
+    lax.fori_loop(0, NB, finish, 0, unroll=2)
 
 
 def shards(conductance, nodata_mask, source_index, source_current, ground_index):

time: 43.1 us -> 42.4 us (0.984)
  Pallas kernels: 41.9 us -> 41.3 us
    pallas_call x1, Pallas kernels: 41.9 us -> 41.3 us  [shards(): pl.pallas_call(body, out_shape=pltpu.VMEM((NB, CR, CC), F32), in_specs=[p...]
where the time goes in v5:
time: 42.4 us; the launch traced here: 42.2 us
  Pallas kernels  41.3 us (97%)
  local copies, waits for them, and re-layouts  0.97 us (2%)
    pallas_call x1, Pallas kernels, shards(): pl.pallas_call(body, out_shape=pltpu.VMEM((NB, CR, CC), F32), in_specs=[p...  41.3 us
    unnamed x1, local copies, waits for them, and re-layouts  0.97 us

profile of v5, /device:TPU:1, one launch (start us, length us, event | category | flops | bytes accessed | tf_op | source)
XLA Modules:
  0.0 42.2 jit_solution(4945655231731810988)
XLA Ops:
  0.0 41.3 %shard_map.55 = f32[16,32,512]{2,1,0:T(8,128)S(1)} custom-call(f32[32,512]{1,0:T(8,128)} %cond_hbm.1, s32[32,512]{1,0:T(8,128)} %mask_hbm.1, s32[16,16]{1,0:T(8,128)} %sidx_hbm.1, f32[16,16]{1,0:T(8,128)} %scur_hbm.1, s32[16,16]{1,0:T(8,128)} %gidx_hbm.1), custom_call_target="tpu_custom_call" | custom-call | tf_op jit(solution)/shard_map/pallas_call | solution.py:719
  41.3 1.0 %copy.7 = f32[16,32,512]{2,1,0:T(8,128)} copy(f32[16,32,512]{2,1,0:T(8,128)S(1)} %shard_map.55) | data formatting | bytes 2097152

commit v6 on v5

--- a/solution.py
+++ b/solution.py
@@ -607,8 +607,8 @@
     y0 = solve(f0)
     combine(v0, s_b, around_field(y0), 11, 1.0 / 81.0)
 
+    send_b(1)
     sweep(v0, s_a, 10, image=w0)
-    send_b(1)
     sweep(s_a, s_b, 9)
     sweep(s_b, s_a, 8)
     sweep(s_a, s_b, 7)

time: 42.4 us -> 43.2 us (1.019)
  Pallas kernels: 41.3 us -> 42.1 us
    pallas_call x1, Pallas kernels: 41.3 us -> 42.1 us  [shards(): pl.pallas_call(body, out_shape=pltpu.VMEM((NB, CR, CC), F32), in_specs=[p...]
where the time goes in v6:
time: 43.2 us; the launch traced here: 43.1 us
  Pallas kernels  42.1 us (97%)
  local copies, waits for them, and re-layouts  0.97 us (2%)
    pallas_call x1, Pallas kernels, shards(): pl.pallas_call(body, out_shape=pltpu.VMEM((NB, CR, CC), F32), in_specs=[p...  42.1 us
    unnamed x1, local copies, waits for them, and re-layouts  0.97 us

profile of v6, /device:TPU:1, one launch (start us, length us, event | category | flops | bytes accessed | tf_op | source)
XLA Modules:
  0.0 43.1 jit_solution(17939118461771722507)
XLA Ops:
  0.0 42.1 %shard_map.55 = f32[16,32,512]{2,1,0:T(8,128)S(1)} custom-call(f32[32,512]{1,0:T(8,128)} %cond_hbm.1, s32[32,512]{1,0:T(8,128)} %mask_hbm.1, s32[16,16]{1,0:T(8,128)} %sidx_hbm.1, f32[16,16]{1,0:T(8,128)} %scur_hbm.1, s32[16,16]{1,0:T(8,128)} %gidx_hbm.1), custom_call_target="tpu_custom_call" | custom-call | tf_op jit(solution)/shard_map/pallas_call | solution.py:719
  42.1 1.0 %copy.7 = f32[16,32,512]{2,1,0:T(8,128)} copy(f32[16,32,512]{2,1,0:T(8,128)S(1)} %shard_map.55) | data formatting | bytes 2097152
